TPU v7x, 32 devices: a whole 2x2x4 slice. The times are simulated.
32 devices in a mesh: seg: 32 (over z, y, x, core).
Axes of the slice: x: 2, y: 2, z: 4, core: 2. Of those that a mesh axis runs over, the one named last changes fastest.
Arguments:
- cam_jac: bfloat16 [18, 512, 512], P(None, 'seg'), may hold values from -0.25 to 0.25
- point_jac: bfloat16 [6, 512, 512], P(None, 'seg'), may hold values from -6 to 6
- obs_point: int32 [512, 512], P('seg'), may hold values from 0 to 1791, as said below
- obs_count: int32 [512], P('seg'), may hold values from 64 to 512, as said below
- back_list: int32 [32, 384], P('seg'), may hold values from 0 to 1023, as said below
- front_list: int32 [32, 384], P('seg'), may hold values from 0 to 1023, as said below
- point_damp: float32 [32768], P('seg'), may hold values from 0.5 to 4
- cam_damp: float32 [512], P('seg'), may hold values from 0.1 to 1
- right_side: float32 [9, 512], P(None, 'seg'), may hold values from -25 to 25
- start_guess: float32 [9, 512], P(None, 'seg'), may hold values from -3 to 3
Outputs:
- camera_step: float32 [9, 512], P(None, 'seg')
- residual: float32 [9, 512], P(None, 'seg')
Inputs may be any that keep to these rules, and one draw needn't show every extreme that they name: `obs_point`: entries below 1024 name the segment's own points; an entry e from 1024 to 1407 names entry e - 1024 of the previous segment's back_list, and a larger one entry e - 1408 of the next segment's front_list. Keyframes of the first segment name no back slot, those of the last segment no front slot. `obs_count`: slots at or past a keyframe's count are padding. Every segment has a keyframe whose slots are all used. `back_list`: each row holds 384 distinct own points of the segment; no point stands on both lists of its segment. `front_list`: each row holds 384 distinct own points of the segment; no point stands on both lists of its segment.
All inputs are finite; a program needn't handle non-finite values.
Results may differ from a plain program's by a relative error of at most 0.0005.
Values sent between devices are 32-bit elements; how exact they have to be, the bound alone decides.
A program may use at most 64 MiB of HBM per device.

v0:
```python
import functools

import jax
import jax.numpy as jnp
from jax import lax
from jax.experimental import pallas as pl
from jax.experimental.pallas import tpu as pltpu
from jax.sharding import PartitionSpec as P

ENTRY_PAIRS = ((0, 0), (0, 1), (0, 2), (1, 1), (1, 2), (2, 2))
F32, BF16, I32 = jnp.float32, jnp.bfloat16, jnp.int32
MESH = pl.DeviceIdType.MESH
LANES = 128
WIDE = 256
GROUP = 8
SPLITS = 2
FIRST_ROWS = (0, 9, 12)
LOAD_ORDER = (
    "back_list",
    "front_list",
    "obs_count",
    "obs_point",
    "cam_damp",
    "start_guess",
    "right_side",
    "point_damp",
    "point_jac",
    "cam_jac",
)


def splits_of(value):
    terms = []
    for step in range(SPLITS):
        term = value.astype(BF16).astype(F32)
        terms.append(term)
        value = value - term
    return terms


def iota(shape, dim):
    return lax.broadcasted_iota(I32, shape, dim)


def dot_nt(left, right):
    return lax.dot_general(left, right, (((1,), (1,)), ((), ())), preferred_element_type=F32)


def symmetric_inverse(entries):
    cofactors = [
        entries[3] * entries[5] - entries[4] * entries[4],
        entries[2] * entries[4] - entries[1] * entries[5],
        entries[1] * entries[4] - entries[2] * entries[3],
        entries[0] * entries[5] - entries[2] * entries[2],
        entries[1] * entries[2] - entries[0] * entries[4],
        entries[0] * entries[3] - entries[1] * entries[1],
    ]
    determinant = entries[0] * cofactors[0] + entries[1] * cofactors[1] + entries[2] * cofactors[2]
    determinant = jnp.where(determinant > 0.0, determinant, 1.0)
    return [member / determinant for member in cofactors]


def apply_inverse(inverse, sums):
    return [
        inverse[0] * sums[0] + inverse[1] * sums[1] + inverse[2] * sums[2],
        inverse[1] * sums[0] + inverse[3] * sums[1] + inverse[4] * sums[2],
        inverse[2] * sums[0] + inverse[4] * sums[1] + inverse[5] * sums[2],
    ]


def kernel(
    n,
    cam_jac_hbm,
    point_jac_hbm,
    obs_point_hbm,
    obs_count_hbm,
    back_list_hbm,
    front_list_hbm,
    point_damp_hbm,
    cam_damp_hbm,
    right_side_hbm,
    start_guess_hbm,
    step_out,
    residual_out,
    lane_hot,
    spread,
    group_of,
    picked,
    to_next,
    to_prev,
    from_prev,
    from_next,
    dots_out,
    dots_in,
    next_send,
    next_recv,
    prev_send,
    prev_recv,
    dots_send,
    dots_recv,
    cam_jac,
    point_jac,
    obs_point,
    obs_count,
    back_list,
    front_list,
    point_damp,
    cam_damp,
    right_side,
    start_guess,
    load_sem,
):
    cams, slots = obs_point.shape
    points = point_damp.shape[1]
    border = back_list.shape[1]
    edge = border // LANES
    own_groups = points // WIDE
    me = lax.axis_index("seg")

    loads = {
        "cam_jac": pltpu.make_async_copy(cam_jac_hbm, cam_jac, load_sem.at[0]),
        "point_jac": pltpu.make_async_copy(point_jac_hbm, point_jac, load_sem.at[1]),
        "obs_point": pltpu.make_async_copy(obs_point_hbm, obs_point, load_sem.at[2]),
        "obs_count": pltpu.make_async_copy(obs_count_hbm, obs_count, load_sem.at[3]),
        "back_list": pltpu.make_async_copy(back_list_hbm, back_list, load_sem.at[4]),
        "front_list": pltpu.make_async_copy(front_list_hbm, front_list, load_sem.at[5]),
        "point_damp": pltpu.make_async_copy(point_damp_hbm, point_damp, load_sem.at[6]),
        "cam_damp": pltpu.make_async_copy(cam_damp_hbm, cam_damp, load_sem.at[7]),
        "right_side": pltpu.make_async_copy(right_side_hbm, right_side, load_sem.at[8]),
        "start_guess": pltpu.make_async_copy(start_guess_hbm, start_guess, load_sem.at[9]),
    }
    for name in LOAD_ORDER:
        loads[name].start()

    barrier = pltpu.get_barrier_semaphore()

    def greet(offset, carry):
        pl.semaphore_signal(
            barrier, inc=1, device_id=(lax.rem(me + offset, n),), device_id_type=MESH
        )
        return carry

    from_prev[...] = jnp.zeros_like(from_prev)
    from_next[...] = jnp.zeros_like(from_next)
    lax.fori_loop(1, n, greet, 0)

    loads["back_list"].wait()
    loads["front_list"].wait()
    listed = jnp.concatenate([back_list[...], front_list[...]], axis=1)
    total = 2 * border
    place = iota((1, total), 1)
    in_front = place >= border
    place = jnp.where(in_front, place - border, place)
    list_group = jnp.where(in_front, edge, 0) + lax.shift_right_logical(place, 7)
    list_lane = jnp.where(in_front, LANES, 0) + (place & (LANES - 1))
    row = iota((2 * own_groups, total), 0)
    code = jnp.where(row < own_groups, list_group + 1, list_lane)
    wanted = jnp.where(row < own_groups, row, row - own_groups)
    code = jnp.where(lax.shift_right_logical(listed, 8) == wanted, code, 0)
    hot = jnp.where(iota((WIDE, total), 0) == (listed & (WIDE - 1)), 1.0, 0.0).astype(BF16)
    table = dot_nt(code.astype(F32).astype(BF16), hot)
    table_group = table[:own_groups]
    table_lane = table[own_groups:]
    other = jnp.where(table_group == 0.0, 1.0, 0.0)
    before = jnp.where(iota((WIDE, WIDE), 0) < iota((WIDE, WIDE), 1), 1.0, 0.0).astype(BF16)
    rank = jnp.dot(other.astype(BF16), before, preferred_element_type=F32)
    counts = jnp.sum(other, axis=1, keepdims=True)
    table_row = iota((own_groups, WIDE), 0)
    for index in range(own_groups - 1):
        rank = rank + jnp.where(table_row > index, counts[index : index + 1], 0.0)
    rank = rank.astype(I32)
    is_other = other > 0.0
    table_group = jnp.where(
        is_other, (2 * edge + lax.shift_right_logical(rank, 8)).astype(F32), table_group - 1.0
    )
    table_lane = jnp.where(is_other, (rank & (WIDE - 1)).astype(F32), table_lane)
    table = jnp.concatenate([table_group, table_lane], axis=0).astype(BF16)

    eye = iota((cams, cams), 0) == iota((cams, cams), 1)

    def column(line):
        wide = jnp.broadcast_to(line, (cams, cams))
        return jnp.sum(jnp.where(eye, wide, jnp.zeros_like(wide)), axis=1, keepdims=True)

    def line(col):
        wide = jnp.broadcast_to(col, (cams, cams))
        return jnp.sum(jnp.where(eye, wide, 0.0), axis=0, keepdims=True)

    loads["obs_count"].wait()
    loads["obs_point"].wait()
    used_count = column(obs_count[...].astype(F32)).astype(I32)
    used = iota((cams, slots), 1) < used_count

    ids = obs_point[...]
    back_slot = ids - points
    front_slot = back_slot - border
    own = ids < points
    in_back = ids < points + border
    side_group = jnp.where(
        in_back, lax.shift_right_logical(back_slot, 7), edge + lax.shift_right_logical(front_slot, 7)
    )
    side_lane = jnp.where(
        in_back, LANES + (back_slot & (LANES - 1)), front_slot & (LANES - 1)
    )
    old_group = lax.shift_right_logical(ids, 8)
    old_lane = ids & (WIDE - 1)
    wide_row = iota((WIDE, slots), 0)
    look_row = iota((2 * own_groups, slots), 0)
    look_row = jnp.where(look_row < own_groups, look_row, look_row - own_groups)
    for cam in range(cams):
        pick = slice(cam, cam + 1)
        hot = jnp.where(wide_row == old_lane[pick], 1.0, 0.0).astype(BF16)
        found = jnp.dot(table, hot, preferred_element_type=F32)
        found = jnp.where(look_row == old_group[pick], found, 0.0)
        new_group = jnp.sum(found[:own_groups], axis=0, keepdims=True).astype(I32)
        new_lane = jnp.sum(found[own_groups:], axis=0, keepdims=True).astype(I32)
        new_group = jnp.where(own[pick], new_group, side_group[pick])
        new_lane = jnp.where(own[pick], new_lane, side_lane[pick])
        group_of[pick] = jnp.where(used[pick], new_group, -1)
        lane_hot[:, cam * slots : (cam + 1) * slots] = jnp.where(
            wide_row == new_lane, 1.0, 0.0
        ).astype(BF16)

    group_row = iota((GROUP, slots), 0)

    def point_sums(values):
        rows = len(values) * GROUP
        terms = [splits_of(value) for value in values]
        for cam in range(cams):
            mask = group_row == group_of[cam : cam + 1]
            blocks = [
                jnp.where(mask, terms[index][step][cam : cam + 1], 0.0)
                for step in range(SPLITS)
                for index in range(len(values))
            ]
            spread[: SPLITS * rows, cam * slots : (cam + 1) * slots] = jnp.concatenate(
                blocks, axis=0
            ).astype(BF16)
        sums = dot_nt(spread[: SPLITS * rows], lane_hot[...])
        whole = sums[(SPLITS - 1) * rows :]
        for step in reversed(range(SPLITS - 1)):
            whole = whole + sums[step * rows : (step + 1) * rows]
        return [whole[index * GROUP : (index + 1) * GROUP] for index in range(len(values))]

    def neighbour(where, turn, size):
        spot = FIRST_ROWS[turn]
        if where == "next":
            return pltpu.make_async_remote_copy(
                src_ref=to_next.at[pl.ds(spot, size)],
                dst_ref=from_prev.at[pl.ds(spot, size)],
                send_sem=next_send.at[turn],
                recv_sem=next_recv.at[turn],
                device_id=(lax.rem(me + 1, n),),
                device_id_type=MESH,
            )
        return pltpu.make_async_remote_copy(
            src_ref=to_prev.at[pl.ds(spot, size)],
            dst_ref=from_next.at[pl.ds(spot, size)],
            send_sem=prev_send.at[turn],
            recv_sem=prev_recv.at[turn],
            device_id=(lax.rem(me + n - 1, n),),
            device_id_type=MESH,
        )

    has_next = me < n - 1
    has_prev = me > 0

    def send(sums, turn):
        spot = FIRST_ROWS[turn]
        for index, member in enumerate(sums):
            to_next[spot + index] = member[:, :LANES]
            to_prev[spot + index] = member[:, LANES:]

        @pl.when(has_next)
        def _():
            neighbour("next", turn, len(sums)).start()

        @pl.when(has_prev)
        def _():
            neighbour("prev", turn, len(sums)).start()

    edge_row = iota((GROUP, LANES), 0) < 2 * edge

    def receive(sums, turn):
        spot = FIRST_ROWS[turn]
        @pl.when(has_next)
        def _():
            copy = neighbour("next", turn, len(sums))
            copy.wait_send()
            neighbour("prev", turn, len(sums)).wait_recv()

        @pl.when(has_prev)
        def _():
            copy = neighbour("prev", turn, len(sums))
            copy.wait_send()
            neighbour("next", turn, len(sums)).wait_recv()

        return [
            jnp.concatenate(
                [
                    member[:, :LANES] + jnp.where(edge_row, from_next[spot + index], 0.0),
                    member[:, LANES:] + jnp.where(edge_row, from_prev[spot + index], 0.0),
                ],
                axis=1,
            )
            for index, member in enumerate(sums)
        ]

    def jac(index):
        return cam_jac[index].astype(F32)

    def pjac(index):
        return point_jac[index].astype(F32)

    def errors_of(vector):
        rows = []
        for side in range(2):
            running = jac(9 * side) * vector[0]
            for entry in range(1, 9):
                running = running + jac(9 * side + entry) * vector[entry]
            rows.append(jnp.where(used, running, 0.0))
        return rows

    def products(errors):
        return [errors[0] * pjac(entry) + errors[1] * pjac(3 + entry) for entry in range(3)]

    def finish(vector, errors, values):
        terms = [splits_of(value) for value in values]
        stacked = jnp.concatenate(
            [terms[index][step] for step in range(SPLITS) for index in range(3)], axis=0
        ).astype(BF16)
        rows = 3 * GROUP
        for cam in range(cams):
            found = jnp.dot(
                stacked,
                lane_hot[:, cam * slots : (cam + 1) * slots],
                preferred_element_type=F32,
            )
            whole = found[(SPLITS - 1) * rows :]
            for step in reversed(range(SPLITS - 1)):
                whole = whole + found[step * rows : (step + 1) * rows]
            mask = group_row == group_of[cam : cam + 1]
            for index in range(3):
                picked[index, cam : cam + 1] = jnp.sum(
                    jnp.where(mask, whole[index * GROUP : (index + 1) * GROUP], 0.0),
                    axis=0,
                    keepdims=True,
                )
        adjusted = []
        for side in range(2):
            back = picked[0] * pjac(3 * side)
            back = back + picked[1] * pjac(3 * side + 1)
            back = back + picked[2] * pjac(3 * side + 2)
            adjusted.append(errors[side] - back)
        return [
            damp * vector[entry]
            + jnp.sum(
                jac(entry) * adjusted[0] + jac(9 + entry) * adjusted[1], axis=1, keepdims=True
            )
            for entry in range(9)
        ]

    def dot_of(left, right):
        running = left[0] * right[0]
        for entry in range(1, 9):
            running = running + left[entry] * right[entry]
        return jnp.sum(running, axis=0, keepdims=True)

    dot_lane = iota((1, LANES), 1)

    def dots_copy(which, offset):
        return pltpu.make_async_remote_copy(
            src_ref=dots_out.at[which],
            dst_ref=dots_in.at[which, offset - 1],
            send_sem=dots_send.at[which],
            recv_sem=dots_recv.at[which],
            device_id=(lax.rem(me + offset, n),),
            device_id_type=MESH,
        )

    def send_dots(which, members):
        packed = jnp.zeros((1, LANES), F32)
        for index, member in enumerate(members):
            packed = jnp.where(dot_lane == index, member, packed)
        dots_out[which] = packed

        def one(offset, carry):
            dots_copy(which, offset).start()
            return carry

        lax.fori_loop(1, n, one, 0)
        return packed

    def receive_dots(which, packed, count):
        pltpu.make_async_copy(dots_in.at[which], dots_in.at[which], dots_recv.at[which]).wait()
        pltpu.make_async_copy(dots_in.at[which], dots_in.at[which], dots_send.at[which]).wait()
        whole = packed + jnp.sum(dots_in[which], axis=0)
        return [
            jnp.sum(jnp.where(dot_lane == index, whole, 0.0), axis=1, keepdims=True)
            for index in range(count)
        ]

    for name in LOAD_ORDER[4:]:
        loads[name].wait()
    damp = column(cam_damp[...])
    start = [column(start_guess[entry : entry + 1]) for entry in range(9)]
    right = [column(right_side[entry : entry + 1]) for entry in range(9)]

    errors = errors_of(start)
    blocks = [
        pjac(lead) * pjac(tail) + pjac(3 + lead) * pjac(3 + tail) for lead, tail in ENTRY_PAIRS
    ]
    sums = point_sums(blocks + products(errors))

    damping = jnp.zeros((SPLITS * GROUP, WIDE), F32)
    damp_row = iota((GROUP, WIDE), 0)
    square_row = iota((WIDE, WIDE), 0)
    for index in range(own_groups):
        here = point_damp[:, index * WIDE : (index + 1) * WIDE]
        mask = damp_row == table_group[index : index + 1].astype(I32)
        block = jnp.concatenate([jnp.where(mask, term, 0.0) for term in splits_of(here)], axis=0)
        hot = jnp.where(
            square_row == table_lane[index : index + 1].astype(I32), 1.0, 0.0
        ).astype(BF16)
        damping = damping + dot_nt(block.astype(BF16), hot)
    moved = damping[(SPLITS - 1) * GROUP :]
    for step in reversed(range(SPLITS - 1)):
        moved = moved + damping[step * GROUP : (step + 1) * GROUP]
    for index, (lead, tail) in enumerate(ENTRY_PAIRS):
        if lead == tail:
            sums[index] = sums[index] + moved

    pl.semaphore_wait(barrier, n - 1)
    send(sums, 0)

    precond = []
    for entry in range(9):
        squared = jnp.where(used, jac(entry) ** 2 + jac(9 + entry) ** 2, 0.0)
        precond.append(1.0 / (jnp.sum(squared, axis=1, keepdims=True) + damp))

    sums = receive(sums, 0)
    inverse = symmetric_inverse(sums[:6])
    image = finish(start, errors, apply_inverse(inverse, sums[6:]))
    residual = [right[entry] - image[entry] for entry in range(9)]
    direction = [precond[entry] * residual[entry] for entry in range(9)]

    errors = errors_of(direction)
    sums = point_sums(products(errors))
    send(sums, 1)
    sums = receive(sums, 1)
    values = apply_inverse(inverse, sums)
    image = finish(direction, errors, values)

    first = send_dots(0, [dot_of(residual, direction), dot_of(direction, image)])
    ahead = [precond[entry] * image[entry] for entry in range(9)]
    errors_ahead = errors_of(ahead)
    sums_ahead = point_sums(products(errors_ahead))
    send(sums_ahead, 2)
    sums_ahead = receive(sums_ahead, 2)
    values_ahead = apply_inverse(inverse, sums_ahead)

    inner, curve = receive_dots(0, first, 2)
    step = inner / curve
    solution = [start[entry] + step * direction[entry] for entry in range(9)]
    residual = [residual[entry] - step * image[entry] for entry in range(9)]
    scaled = [precond[entry] * residual[entry] for entry in range(9)]

    quadratic = jnp.zeros((cams, 1), F32)
    for entry in range(9):
        quadratic = quadratic + damp * scaled[entry] * scaled[entry]
    squares = (errors[0] - step * errors_ahead[0]) ** 2 + (errors[1] - step * errors_ahead[1]) ** 2
    quadratic = quadratic + jnp.sum(squares, axis=1, keepdims=True)
    quadratic = jnp.sum(quadratic, axis=0, keepdims=True)
    point_part = jnp.zeros((GROUP, WIDE), F32)
    for index in range(3):
        point_part = point_part + (sums[index] - step * sums_ahead[index]) * (
            values[index] - step * values_ahead[index]
        )
    part_row = iota((GROUP, WIDE), 0)
    part_left = iota((GROUP, WIDE), 1) < LANES
    own_row = jnp.where(part_left, part_row, part_row - edge)
    is_own = jnp.where(part_left, edge - 1 - own_row, own_row) >= 0
    is_own = is_own | (part_row >= 2 * edge)
    point_part = jnp.sum(jnp.where(is_own, point_part, 0.0), axis=1, keepdims=True)
    quadratic = quadratic - jnp.sum(point_part, axis=0, keepdims=True)
    second = send_dots(1, [dot_of(residual, scaled), quadratic, dot_of(scaled, image)])

    further = finish(ahead, errors_ahead, values_ahead)
    applied = [image[entry] - step * further[entry] for entry in range(9)]
    inner_next, own_curve, cross = receive_dots(1, second, 3)
    ratio = inner_next / inner
    curve = own_curve + ratio * (2.0 * cross + ratio * curve)
    step = inner_next / curve
    for entry in range(9):
        fresh = scaled[entry] + ratio * direction[entry]
        seen = applied[entry] + ratio * image[entry]
        step_out[entry : entry + 1] = line(solution[entry] + step * fresh)
        residual_out[entry : entry + 1] = line(residual[entry] - step * seen)


def solution(mesh):
    n = mesh.shape["seg"]

    def shards(
        cam_jac,
        point_jac,
        obs_point,
        obs_count,
        back_list,
        front_list,
        point_damp,
        cam_damp,
        right_side,
        start_guess,
    ):
        cams, slots = obs_point.shape
        observations = cams * slots
        operands = (
            cam_jac,
            point_jac,
            obs_point,
            obs_count.reshape(1, -1),
            back_list,
            front_list,
            point_damp.reshape(1, -1),
            cam_damp.reshape(1, -1),
            right_side,
            start_guess,
        )
        vector = jax.ShapeDtypeStruct(right_side.shape, F32)
        return pl.pallas_call(
            functools.partial(kernel, n),
            out_shape=(vector, vector),
            in_specs=[pl.BlockSpec(memory_space=pltpu.HBM)] * 10,
            out_specs=(pl.BlockSpec(memory_space=pltpu.VMEM),) * 2,
            scratch_shapes=[
                pltpu.VMEM((WIDE, observations), BF16),
                pltpu.VMEM((SPLITS * 9 * GROUP, observations), BF16),
                pltpu.VMEM((cams, slots), I32),
                pltpu.VMEM((3, cams, slots), F32),
                pltpu.VMEM((15, GROUP, LANES), F32),
                pltpu.VMEM((15, GROUP, LANES), F32),
                pltpu.VMEM((15, GROUP, LANES), F32),
                pltpu.VMEM((15, GROUP, LANES), F32),
                pltpu.VMEM((2, 1, LANES), F32),
                pltpu.VMEM((2, n - 1, 1, LANES), F32),
                pltpu.SemaphoreType.DMA((3,)),
                pltpu.SemaphoreType.DMA((3,)),
                pltpu.SemaphoreType.DMA((3,)),
                pltpu.SemaphoreType.DMA((3,)),
                pltpu.SemaphoreType.DMA((2,)),
                pltpu.SemaphoreType.DMA((2,)),
                *[pltpu.VMEM(member.shape, member.dtype) for member in operands],
                pltpu.SemaphoreType.DMA((len(operands),)),
            ],
            compiler_params=pltpu.CompilerParams(
                collective_id=0, has_side_effects=True, vmem_limit_bytes=56 * 1024 * 1024
            ),
            name="schur_cg",
        )(*operands)

    return jax.shard_map(
        shards,
        mesh=mesh,
        in_specs=(
            P(None, "seg", None),
            P(None, "seg", None),
            P("seg", None),
            P("seg"),
            P("seg", None),
            P("seg", None),
            P("seg"),
            P("seg"),
            P(None, "seg"),
            P(None, "seg"),
        ),
        out_specs=(P(None, "seg"), P(None, "seg")),
        check_vma=False,
    )
```

profile of v0, /device:TPU:0, one launch (start us, length us, event | category | flops | bytes accessed | tf_op | source)
XLA Modules:
  0.0 33.8 jit_solution(13172873067423832041)
XLA Ops:
  0.6 31.2 %schur_cg.1 = (f32[9,16]{1,0:T(8,128)}, f32[9,16]{1,0:T(8,128)}) custom-call(bf16[18,16,512]{2,1,0:T(8,128)(2,1)} %cam_jac_hbm.1, bf16[6,16,512]{2,1,0:T(8,128)(2,1)} %point_jac_hbm.1, s32[16,512]{1,0:T(8,128)} %obs_point_hbm.1, s32[1,16]{1,0:T(1,128)} %bitcast.4, s32[1,384]{1,0:T(1,128)} %back_list_hbm.1, s32[1,384]{1,0:T(1,128)} %front_list_hbm.1, ...), custom_call_target="tpu_custom_call" | custom-call | tf_op jit(solution)/shard_map/schur_cg/pallas_call | solution.py:531
  31.9 0.0 copy-start
  31.9 1.3 %copy.14 = f32[9,16]{1,0:T(8,128)} copy(f32[9,16]{1,0:T(8,128)} %get-tuple-element.4) | data formatting | bytes 1152
  33.2 0.0 copy-done
  33.2 0.6 %copy.15 = f32[9,16]{1,0:T(8,128)} copy(f32[9,16]{1,0:T(8,128)S(1)} %copy-done) | data formatting | bytes 1152
Async XLA Ops:
  31.9 1.3 %copy-start = (f32[9,16]{1,0:T(8,128)S(1)}, f32[9,16]{1,0:T(8,128)}, u32[]{:S(2)}) copy-start(f32[9,16]{1,0:T(8,128)} %get-tuple-element.5) | copy-start | bytes 1732
where the time goes:
time: 33.9 us; the launch traced here: 33.8 us
  Pallas kernels  31.2 us (92%)
  local copies, waits for them, and re-layouts  1.9 us (6%)
  between operations  0.65 us (2%)
    pallas_call x1, Pallas kernels, shards(): pl.pallas_call(functools.partial(kernel, n), out_shape=(vector, vector),...  31.2 us
    unnamed x4, local copies, waits for them, and re-layouts  1.9 us

commit v1 on v0

v1 whole, which is shorter than its diff:
```python
import functools

import jax
import jax.numpy as jnp
from jax import lax
from jax.experimental import pallas as pl
from jax.experimental.pallas import tpu as pltpu
from jax.sharding import PartitionSpec as P

ENTRY_PAIRS = ((0, 0), (0, 1), (0, 2), (1, 1), (1, 2), (2, 2))
F32, BF16, I32 = jnp.float32, jnp.bfloat16, jnp.int32
MESH = pl.DeviceIdType.MESH
LANES = 128
WIDE = 256
GROUP = 8
SPLITS = 2
FIRST_ROWS = (0, 9, 12)
SQUARES = tuple((lead, tail) for lead in range(9) for tail in range(lead, 9))
LOAD_ORDER = (
    "back_list",
    "front_list",
    "obs_count",
    "obs_point",
    "cam_damp",
    "start_guess",
    "right_side",
    "point_damp",
    "point_jac",
    "cam_jac",
)


def splits_of(value):
    terms = []
    for step in range(SPLITS):
        term = value.astype(BF16).astype(F32)
        terms.append(term)
        value = value - term
    return terms


def iota(shape, dim):
    return lax.broadcasted_iota(I32, shape, dim)


def dot_nt(left, right):
    return lax.dot_general(left, right, (((1,), (1,)), ((), ())), preferred_element_type=F32)


def symmetric_inverse(entries):
    cofactors = [
        entries[3] * entries[5] - entries[4] * entries[4],
        entries[2] * entries[4] - entries[1] * entries[5],
        entries[1] * entries[4] - entries[2] * entries[3],
        entries[0] * entries[5] - entries[2] * entries[2],
        entries[1] * entries[2] - entries[0] * entries[4],
        entries[0] * entries[3] - entries[1] * entries[1],
    ]
    determinant = entries[0] * cofactors[0] + entries[1] * cofactors[1] + entries[2] * cofactors[2]
    determinant = jnp.where(determinant > 0.0, determinant, 1.0)
    return [member / determinant for member in cofactors]


def apply_inverse(inverse, sums):
    return [
        inverse[0] * sums[0] + inverse[1] * sums[1] + inverse[2] * sums[2],
        inverse[1] * sums[0] + inverse[3] * sums[1] + inverse[4] * sums[2],
        inverse[2] * sums[0] + inverse[4] * sums[1] + inverse[5] * sums[2],
    ]


def kernel(
    n,
    cam_jac_hbm,
    point_jac_hbm,
    obs_point_hbm,
    obs_count_hbm,
    back_list_hbm,
    front_list_hbm,
    point_damp_hbm,
    cam_damp_hbm,
    right_side_hbm,
    start_guess_hbm,
    step_out,
    residual_out,
    group_of,
    lane_of,
    wide_jac,
    first_terms,
    terms,
    coupling,
    partial,
    vector_rows,
    squares,
    to_next,
    to_prev,
    from_prev,
    from_next,
    dots_out,
    dots_in,
    next_send,
    next_recv,
    prev_send,
    prev_recv,
    dots_send,
    dots_recv,
    cam_jac,
    point_jac,
    obs_point,
    obs_count,
    back_list,
    front_list,
    point_damp,
    cam_damp,
    right_side,
    start_guess,
    load_sem,
):
    cams, slots = obs_point.shape
    points = point_damp.shape[1]
    border = back_list.shape[1]
    edge = border // LANES
    own_groups = points // WIDE
    halves = WIDE // LANES
    me = lax.axis_index("seg")

    loads = {
        "cam_jac": pltpu.make_async_copy(cam_jac_hbm, cam_jac, load_sem.at[0]),
        "point_jac": pltpu.make_async_copy(point_jac_hbm, point_jac, load_sem.at[1]),
        "obs_point": pltpu.make_async_copy(obs_point_hbm, obs_point, load_sem.at[2]),
        "obs_count": pltpu.make_async_copy(obs_count_hbm, obs_count, load_sem.at[3]),
        "back_list": pltpu.make_async_copy(back_list_hbm, back_list, load_sem.at[4]),
        "front_list": pltpu.make_async_copy(front_list_hbm, front_list, load_sem.at[5]),
        "point_damp": pltpu.make_async_copy(point_damp_hbm, point_damp, load_sem.at[6]),
        "cam_damp": pltpu.make_async_copy(cam_damp_hbm, cam_damp, load_sem.at[7]),
        "right_side": pltpu.make_async_copy(right_side_hbm, right_side, load_sem.at[8]),
        "start_guess": pltpu.make_async_copy(start_guess_hbm, start_guess, load_sem.at[9]),
    }
    for name in LOAD_ORDER:
        loads[name].start()

    barrier = pltpu.get_barrier_semaphore()

    def greet(offset, carry):
        pl.semaphore_signal(
            barrier, inc=1, device_id=(lax.rem(me + offset, n),), device_id_type=MESH
        )
        return carry

    from_prev[...] = jnp.zeros_like(from_prev)
    from_next[...] = jnp.zeros_like(from_next)
    lax.fori_loop(1, n, greet, 0)

    loads["back_list"].wait()
    loads["front_list"].wait()
    listed = jnp.concatenate([back_list[...], front_list[...]], axis=1)
    total = 2 * border
    place = iota((1, total), 1)
    in_front = place >= border
    place = jnp.where(in_front, place - border, place)
    list_group = jnp.where(in_front, edge, 0) + lax.shift_right_logical(place, 7)
    list_lane = jnp.where(in_front, LANES, 0) + (place & (LANES - 1))
    row = iota((2 * own_groups, total), 0)
    code = jnp.where(row < own_groups, list_group + 1, list_lane)
    wanted = jnp.where(row < own_groups, row, row - own_groups)
    code = jnp.where(lax.shift_right_logical(listed, 8) == wanted, code, 0)
    hot = jnp.where(iota((WIDE, total), 0) == (listed & (WIDE - 1)), 1.0, 0.0).astype(BF16)
    table = dot_nt(code.astype(F32).astype(BF16), hot)
    table_group = table[:own_groups]
    table_lane = table[own_groups:]
    other = jnp.where(table_group == 0.0, 1.0, 0.0)
    before = jnp.where(iota((WIDE, WIDE), 0) < iota((WIDE, WIDE), 1), 1.0, 0.0).astype(BF16)
    rank = jnp.dot(other.astype(BF16), before, preferred_element_type=F32)
    counts = jnp.sum(other, axis=1, keepdims=True)
    table_row = iota((own_groups, WIDE), 0)
    for index in range(own_groups - 1):
        rank = rank + jnp.where(table_row > index, counts[index : index + 1], 0.0)
    rank = rank.astype(I32)
    is_other = other > 0.0
    table_group = jnp.where(
        is_other, (2 * edge + lax.shift_right_logical(rank, 8)).astype(F32), table_group - 1.0
    )
    table_lane = jnp.where(is_other, (rank & (WIDE - 1)).astype(F32), table_lane)

    eye = iota((cams, cams), 0) == iota((cams, cams), 1)

    def column(line):
        wide = jnp.broadcast_to(line, (cams, cams))
        return jnp.sum(jnp.where(eye, wide, jnp.zeros_like(wide)), axis=1, keepdims=True)

    def line(wide):
        return jnp.sum(jnp.where(eye, wide[:, :cams], 0.0), axis=0, keepdims=True)

    loads["obs_count"].wait()
    loads["obs_point"].wait()
    used_count = column(obs_count[...].astype(F32)).astype(I32)
    used = iota((cams, slots), 1) < used_count

    code_table = (table_group * WIDE + table_lane).astype(I32)
    rows_of_table = [
        jnp.broadcast_to(
            code_table[index // halves : index // halves + 1, part * LANES : (part + 1) * LANES],
            (GROUP, LANES),
        )
        for index in range(own_groups * halves)
        for part in (index % halves,)
    ]
    for top in range(0, cams, GROUP):
        for left in range(0, slots, LANES):
            spot = (slice(top, top + GROUP), slice(left, left + LANES))
            ids = obs_point[spot]
            back_slot = ids - points
            front_slot = back_slot - border
            in_back = ids < points + border
            side = jnp.where(
                in_back,
                lax.shift_right_logical(back_slot, 7) * WIDE + LANES + (back_slot & (LANES - 1)),
                (edge + lax.shift_right_logical(front_slot, 7)) * WIDE + (front_slot & (LANES - 1)),
            )
            id_row = lax.shift_right_logical(ids, 7)
            id_lane = ids & (LANES - 1)
            for index, row in enumerate(rows_of_table):
                found = jnp.take_along_axis(row, id_lane, axis=1, mode="promise_in_bounds")
                side = jnp.where(id_row == index, found, side)
            group_of[spot] = jnp.where(used[spot], lax.shift_right_logical(side, 8), -1)
            lane_of[spot] = side & (WIDE - 1)

    wide_row = iota((WIDE, slots), 0)
    group_row = iota((GROUP, slots), 0)

    def scatter(source, count, cam):
        mask = group_row == group_of[cam : cam + 1]
        blocks = [
            jnp.where(mask, jnp.broadcast_to(source[index, cam : cam + 1], (GROUP, slots)), 0.0)
            for index in range(SPLITS * count)
        ]
        hot = jnp.where(wide_row == lane_of[cam : cam + 1], 1.0, 0.0).astype(BF16)
        return dot_nt(jnp.concatenate(blocks, axis=0).astype(BF16), hot)

    def joined(sums, index):
        whole = sums[(SPLITS * index + SPLITS - 1) * GROUP : (SPLITS * index + SPLITS) * GROUP]
        for step in reversed(range(SPLITS - 1)):
            first = (SPLITS * index + step) * GROUP
            whole = whole + sums[first : first + GROUP]
        return whole

    def neighbour(where, turn, size):
        spot = FIRST_ROWS[turn]
        if where == "next":
            return pltpu.make_async_remote_copy(
                src_ref=to_next.at[pl.ds(spot, size)],
                dst_ref=from_prev.at[pl.ds(spot, size)],
                send_sem=next_send.at[turn],
                recv_sem=next_recv.at[turn],
                device_id=(lax.rem(me + 1, n),),
                device_id_type=MESH,
            )
        return pltpu.make_async_remote_copy(
            src_ref=to_prev.at[pl.ds(spot, size)],
            dst_ref=from_next.at[pl.ds(spot, size)],
            send_sem=prev_send.at[turn],
            recv_sem=prev_recv.at[turn],
            device_id=(lax.rem(me + n - 1, n),),
            device_id_type=MESH,
        )

    has_next = me < n - 1
    has_prev = me > 0

    def send(sums, turn):
        spot = FIRST_ROWS[turn]
        for index, member in enumerate(sums):
            to_next[spot + index] = member[:, :LANES]
            to_prev[spot + index] = member[:, LANES:]

        @pl.when(has_next)
        def _():
            neighbour("next", turn, len(sums)).start()

        @pl.when(has_prev)
        def _():
            neighbour("prev", turn, len(sums)).start()

    edge_row = iota((GROUP, LANES), 0) < 2 * edge

    def receive(sums, turn):
        spot = FIRST_ROWS[turn]
        @pl.when(has_next)
        def _():
            copy = neighbour("next", turn, len(sums))
            copy.wait_send()
            neighbour("prev", turn, len(sums)).wait_recv()

        @pl.when(has_prev)
        def _():
            copy = neighbour("prev", turn, len(sums))
            copy.wait_send()
            neighbour("next", turn, len(sums)).wait_recv()

        return [
            jnp.concatenate(
                [
                    member[:, :LANES] + jnp.where(edge_row, from_next[spot + index], 0.0),
                    member[:, LANES:] + jnp.where(edge_row, from_prev[spot + index], 0.0),
                ],
                axis=1,
            )
            for index, member in enumerate(sums)
        ]

    def pjac(index):
        return point_jac[index].astype(F32)

    def spread_out(col):
        return jnp.broadcast_to(col, (cams, LANES))

    def point_product(vector):
        for entry in range(9):
            vector_rows[entry] = vector[entry]
        running = [[None] * halves for index in range(3)]
        for cam in range(cams):
            for entry in range(9):
                scale = jnp.broadcast_to(vector_rows[entry, cam : cam + 1], (GROUP, LANES))
                for index in range(3):
                    for part in range(halves):
                        block = coupling[
                            cam * 27 + index * 9 + entry, :, part * LANES : (part + 1) * LANES
                        ]
                        term = block * scale
                        before = running[index][part]
                        running[index][part] = term if before is None else before + term
        return [jnp.concatenate(parts, axis=1) for parts in running]

    def camera_product(values):
        for cam in range(cams):
            for entry in range(9):
                whole = None
                for index in range(3):
                    for part in range(halves):
                        lanes = slice(part * LANES, (part + 1) * LANES)
                        term = coupling[cam * 27 + index * 9 + entry, :, lanes] * values[index][:, lanes]
                        whole = term if whole is None else whole + term
                partial[entry, cam * GROUP : (cam + 1) * GROUP] = whole
        result = []
        for entry in range(9):
            whole = partial[entry, pl.ds(0, cams, stride=GROUP)]
            for row in range(1, GROUP):
                whole = whole + partial[entry, pl.ds(row, cams, stride=GROUP)]
            result.append(spread_out(jnp.sum(whole, axis=1, keepdims=True)))
        return result

    def square_product(vector):
        result = [None] * 9
        for index, (lead, tail) in enumerate(SQUARES):
            block = squares[index]
            for here, there in {(lead, tail), (tail, lead)}:
                term = block * vector[there]
                result[here] = term if result[here] is None else result[here] + term
        return result

    def dot_of(left, right):
        running = left[0] * right[0]
        for entry in range(1, 9):
            running = running + left[entry] * right[entry]
        return jnp.sum(running, axis=0, keepdims=True)

    dot_lane = iota((1, LANES), 1)
    part_row = iota((GROUP, WIDE), 0)
    part_left = iota((GROUP, WIDE), 1) < LANES
    own_row = jnp.where(part_left, part_row, part_row - edge)
    is_own = jnp.where(part_left, edge - 1 - own_row, own_row) >= 0
    is_own = is_own | (part_row >= 2 * edge)

    def point_dot(left, right):
        running = left[0] * right[0]
        for index in range(1, 3):
            running = running + left[index] * right[index]
        running = jnp.where(is_own, running, 0.0)
        running = running[:, :LANES] + running[:, LANES:]
        running = jnp.sum(running, axis=0, keepdims=True)
        return jnp.broadcast_to(jnp.sum(running, axis=1, keepdims=True), (1, LANES))

    def dots_copy(offset):
        return pltpu.make_async_remote_copy(
            src_ref=dots_out,
            dst_ref=dots_in.at[offset - 1],
            send_sem=dots_send,
            recv_sem=dots_recv,
            device_id=(lax.rem(me + offset, n),),
            device_id_type=MESH,
        )

    def start_dots(offset, carry):
        dots_copy(offset).start()
        return carry

    for name in LOAD_ORDER[4:]:
        loads[name].wait()
    damp = column(cam_damp[...])
    start_col = [column(start_guess[entry : entry + 1]) for entry in range(9)]
    right = [spread_out(column(right_side[entry : entry + 1])) for entry in range(9)]
    start = [spread_out(member) for member in start_col]

    for index in range(18):
        wide_jac[index] = jnp.where(used, cam_jac[index].astype(F32), 0.0)
    errors = []
    for side in range(2):
        running = wide_jac[9 * side] * start_col[0]
        for entry in range(1, 9):
            running = running + wide_jac[9 * side + entry] * start_col[entry]
        errors.append(running)
    blocks = [
        pjac(lead) * pjac(tail) + pjac(3 + lead) * pjac(3 + tail) for lead, tail in ENTRY_PAIRS
    ]
    blocks = blocks + [
        errors[0] * pjac(entry) + errors[1] * pjac(3 + entry) for entry in range(3)
    ]
    for index, block in enumerate(blocks):
        for step, term in enumerate(splits_of(block)):
            first_terms[SPLITS * index + step] = term
    whole = scatter(first_terms, 9, 0)
    for cam in range(1, cams):
        whole = whole + scatter(first_terms, 9, cam)
    sums = [joined(whole, index) for index in range(9)]

    damping = jnp.zeros((SPLITS * GROUP, WIDE), F32)
    damp_row = iota((GROUP, WIDE), 0)
    square_row = iota((WIDE, WIDE), 0)
    for index in range(own_groups):
        here = point_damp[:, index * WIDE : (index + 1) * WIDE]
        mask = damp_row == table_group[index : index + 1].astype(I32)
        block = jnp.concatenate([jnp.where(mask, term, 0.0) for term in splits_of(here)], axis=0)
        hot = jnp.where(
            square_row == table_lane[index : index + 1].astype(I32), 1.0, 0.0
        ).astype(BF16)
        damping = damping + dot_nt(block.astype(BF16), hot)
    moved = damping[(SPLITS - 1) * GROUP :]
    for step in reversed(range(SPLITS - 1)):
        moved = moved + damping[step * GROUP : (step + 1) * GROUP]
    for index, (lead, tail) in enumerate(ENTRY_PAIRS):
        if lead == tail:
            sums[index] = sums[index] + moved

    pl.semaphore_wait(barrier, n - 1)
    send(sums, 0)

    for top in range(0, cams, GROUP):
        for left in range(0, slots, LANES):
            spot = (slice(top, top + GROUP), slice(left, left + LANES))
            camera = [wide_jac[(index, *spot)] for index in range(18)]
            for index in range(3):
                one = point_jac[(index, slice(None), spot[1])].astype(F32)[spot[0]]
                two = point_jac[(3 + index, slice(None), spot[1])].astype(F32)[spot[0]]
                for entry in range(9):
                    product = one * camera[entry] + two * camera[9 + entry]
                    for step, term in enumerate(splits_of(product)):
                        terms[(SPLITS * (index * 9 + entry) + step, *spot)] = term
    for cam in range(cams):
        whole = scatter(terms, 27, cam)
        for index in range(27):
            coupling[cam * 27 + index] = joined(whole, index)

    precond = []
    for index, (lead, tail) in enumerate(SQUARES):
        running = None
        for left in range(0, slots, LANES):
            lanes = slice(left, left + LANES)
            term = (
                wide_jac[lead, :, lanes] * wide_jac[tail, :, lanes]
                + wide_jac[9 + lead, :, lanes] * wide_jac[9 + tail, :, lanes]
            )
            running = term if running is None else running + term
        total = jnp.sum(running, axis=1, keepdims=True)
        if lead == tail:
            total = total + damp
            precond.append(spread_out(1.0 / total))
        squares[index] = spread_out(total)
    image = square_product(start)

    sums = receive(sums, 0)
    inverse = symmetric_inverse(sums[:6])
    back = camera_product(apply_inverse(inverse, sums[6:]))
    residual = [right[entry] - (image[entry] - back[entry]) for entry in range(9)]
    direction = [precond[entry] * residual[entry] for entry in range(9)]

    sums = point_product(direction)
    send(sums, 1)
    square_direction = square_product(direction)
    sums = receive(sums, 1)
    values = apply_inverse(inverse, sums)
    back = camera_product(values)
    image = [square_direction[entry] - back[entry] for entry in range(9)]
    ahead = [precond[entry] * image[entry] for entry in range(9)]

    sums_ahead = point_product(ahead)
    send(sums_ahead, 2)
    square_ahead = square_product(ahead)
    inner = dot_of(residual, direction)
    curve = dot_of(direction, image)
    weight = dot_of(image, ahead)
    shift = dot_of(residual, ahead) / jnp.where(weight > 0.0, weight, 1.0)
    shift = jnp.clip(shift, -1e6, 1e6)
    rest = [direction[entry] - shift * ahead[entry] for entry in range(9)]
    left_over = [residual[entry] - shift * image[entry] for entry in range(9)]
    square_rest = [square_direction[entry] - shift * square_ahead[entry] for entry in range(9)]
    members = [
        inner,
        curve,
        dot_of(left_over, rest),
        dot_of(rest, square_rest),
        dot_of(rest, image),
        2.0 * dot_of(left_over, ahead),
        2.0 * dot_of(rest, square_ahead),
        weight,
        weight,
        dot_of(ahead, square_ahead),
    ]
    packed = jnp.zeros((1, LANES), F32)
    for index, member in enumerate(members):
        packed = jnp.where(dot_lane == index, member, packed)
    dots_out[1] = shift
    sums_ahead = receive(sums_ahead, 2)
    values_ahead = apply_inverse(inverse, sums_ahead)
    wide_shift = jnp.concatenate([shift] * halves, axis=1)
    sums_rest = [sums[index] - wide_shift * sums_ahead[index] for index in range(3)]
    values_rest = [values[index] - wide_shift * values_ahead[index] for index in range(3)]
    packed = packed - jnp.where(dot_lane == 3, point_dot(sums_rest, values_rest), 0.0)
    packed = packed - jnp.where(dot_lane == 6, 2.0 * point_dot(sums_rest, values_ahead), 0.0)
    packed = packed - jnp.where(dot_lane == 9, point_dot(sums_ahead, values_ahead), 0.0)
    dots_out[0] = packed
    lax.fori_loop(1, n, start_dots, 0)

    back = camera_product(values_ahead)
    further = [square_ahead[entry] - back[entry] for entry in range(9)]

    pltpu.make_async_copy(dots_in, dots_in, dots_recv).wait()
    pltpu.make_async_copy(dots_in, dots_in, dots_send).wait()

    def picked(row, low, high):
        inside = (dot_lane >= low) & (dot_lane < high)
        return jnp.sum(jnp.where(inside, row, 0.0), axis=1, keepdims=True)

    whole = packed + jnp.sum(dots_in[:, 0], axis=0)
    inner = picked(whole, 0, 1)
    curve = picked(whole, 1, 2)
    step = inner / curve

    def moved_by(row, about):
        gap = about - step
        row = jnp.where(dot_lane >= 5, row * gap, row)
        return jnp.where(dot_lane >= 8, row * gap, row)

    whole = moved_by(packed, shift)
    for offset in range(1, n):
        whole = whole + moved_by(dots_in[offset - 1, 0], dots_in[offset - 1, 1])
    one = (dot_lane == 2) | (dot_lane == 5) | (dot_lane == 8)
    two = (dot_lane == 3) | (dot_lane == 6) | (dot_lane == 9)
    three = (dot_lane == 4) | (dot_lane == 7)
    inner_next = jnp.sum(jnp.where(one, whole, 0.0), axis=1, keepdims=True)
    own_curve = jnp.sum(jnp.where(two, whole, 0.0), axis=1, keepdims=True)
    cross = jnp.sum(jnp.where(three, whole, 0.0), axis=1, keepdims=True)
    ratio = inner_next / inner
    curve = own_curve + ratio * (2.0 * cross + ratio * curve)
    second = inner_next / curve
    for entry in range(9):
        scaled = direction[entry] - step * ahead[entry]
        fresh = scaled + ratio * direction[entry]
        seen = image[entry] - step * further[entry] + ratio * image[entry]
        solved = start[entry] + step * direction[entry] + second * fresh
        left = residual[entry] - step * image[entry] - second * seen
        step_out[entry : entry + 1] = line(solved)
        residual_out[entry : entry + 1] = line(left)


def solution(mesh):
    n = mesh.shape["seg"]

    def shards(
        cam_jac,
        point_jac,
        obs_point,
        obs_count,
        back_list,
        front_list,
        point_damp,
        cam_damp,
        right_side,
        start_guess,
    ):
        cams, slots = obs_point.shape
        operands = (
            cam_jac,
            point_jac,
            obs_point,
            obs_count.reshape(1, -1),
            back_list,
            front_list,
            point_damp.reshape(1, -1),
            cam_damp.reshape(1, -1),
            right_side,
            start_guess,
        )
        vector = jax.ShapeDtypeStruct(right_side.shape, F32)
        return pl.pallas_call(
            functools.partial(kernel, n),
            out_shape=(vector, vector),
            in_specs=[pl.BlockSpec(memory_space=pltpu.HBM)] * 10,
            out_specs=(pl.BlockSpec(memory_space=pltpu.VMEM),) * 2,
            scratch_shapes=[
                pltpu.VMEM((cams, slots), I32),
                pltpu.VMEM((cams, slots), I32),
                pltpu.VMEM((18, cams, slots), F32),
                pltpu.VMEM((SPLITS * 9, cams, slots), F32),
                pltpu.VMEM((SPLITS * 27, cams, slots), F32),
                pltpu.VMEM((cams * 27, GROUP, WIDE), F32),
                pltpu.VMEM((9, cams * GROUP, LANES), F32),
                pltpu.VMEM((9, cams, LANES), F32),
                pltpu.VMEM((len(SQUARES), cams, LANES), F32),
                pltpu.VMEM((15, GROUP, LANES), F32),
                pltpu.VMEM((15, GROUP, LANES), F32),
                pltpu.VMEM((15, GROUP, LANES), F32),
                pltpu.VMEM((15, GROUP, LANES), F32),
                pltpu.VMEM((2, 1, LANES), F32),
                pltpu.VMEM((n - 1, 2, 1, LANES), F32),
                pltpu.SemaphoreType.DMA((3,)),
                pltpu.SemaphoreType.DMA((3,)),
                pltpu.SemaphoreType.DMA((3,)),
                pltpu.SemaphoreType.DMA((3,)),
                pltpu.SemaphoreType.DMA,
                pltpu.SemaphoreType.DMA,
                *[pltpu.VMEM(member.shape, member.dtype) for member in operands],
                pltpu.SemaphoreType.DMA((len(operands),)),
            ],
            compiler_params=pltpu.CompilerParams(
                collective_id=0, has_side_effects=True, vmem_limit_bytes=56 * 1024 * 1024
            ),
            name="schur_cg",
        )(*operands)

    return jax.shard_map(
        shards,
        mesh=mesh,
        in_specs=(
            P(None, "seg", None),
            P(None, "seg", None),
            P("seg", None),
            P("seg"),
            P("seg", None),
            P("seg", None),
            P("seg"),
            P("seg"),
            P(None, "seg"),
            P(None, "seg"),
        ),
        out_specs=(P(None, "seg"), P(None, "seg")),
        check_vma=False,
    )
```

time: 33.9 us -> 25.3 us (0.75)
  Pallas kernels: 31.2 us -> 22.6 us
    pallas_call x1, Pallas kernels: 31.2 us -> 22.6 us  [shards(): pl.pallas_call(functools.partial(kernel, n), out_shape=(vector, vector),...]
where the time goes in v1:
time: 25.3 us; the launch traced here: 25.2 us
  Pallas kernels  22.6 us (89%)
  local copies, waits for them, and re-layouts  1.9 us (8%)
  between operations  0.65 us (3%)
    pallas_call x1, Pallas kernels, shards(): pl.pallas_call(functools.partial(kernel, n), out_shape=(vector, vector),...  22.6 us
    unnamed x4, local copies, waits for them, and re-layouts  1.9 us

profile of v1, /device:TPU:0, one launch (start us, length us, event | category | flops | bytes accessed | tf_op | source)
XLA Modules:
  0.0 25.2 jit_solution(18221777618559668122)
XLA Ops:
  0.6 22.6 %schur_cg.1 = (f32[9,16]{1,0:T(8,128)}, f32[9,16]{1,0:T(8,128)}) custom-call(bf16[18,16,512]{2,1,0:T(8,128)(2,1)} %cam_jac_hbm.1, bf16[6,16,512]{2,1,0:T(8,128)(2,1)} %point_jac_hbm.1, s32[16,512]{1,0:T(8,128)} %obs_point_hbm.1, s32[1,16]{1,0:T(1,128)} %bitcast.4, s32[1,384]{1,0:T(1,128)} %back_list_hbm.1, s32[1,384]{1,0:T(1,128)} %front_list_hbm.1, ...), custom_call_target="tpu_custom_call" | custom-call | tf_op jit(solution)/shard_map/schur_cg/pallas_call | solution.py:604
  23.3 0.0 copy-start
  23.3 1.3 %copy.14 = f32[9,16]{1,0:T(8,128)} copy(f32[9,16]{1,0:T(8,128)} %get-tuple-element.4) | data formatting | bytes 1152
  24.6 0.0 copy-done
  24.6 0.6 %copy.15 = f32[9,16]{1,0:T(8,128)} copy(f32[9,16]{1,0:T(8,128)S(1)} %copy-done) | data formatting | bytes 1152
Async XLA Ops:
  23.3 1.3 %copy-start = (f32[9,16]{1,0:T(8,128)S(1)}, f32[9,16]{1,0:T(8,128)}, u32[]{:S(2)}) copy-start(f32[9,16]{1,0:T(8,128)} %get-tuple-element.5) | copy-start | bytes 1732

commit v2 on v1

--- a/solution.py
+++ b/solution.py
@@ -81,8 +81,7 @@
     cam_damp_hbm,
     right_side_hbm,
     start_guess_hbm,
-    step_out,
-    residual_out,
+    packed_out,
     group_of,
     lane_of,
     wide_jac,
@@ -104,6 +103,7 @@
     prev_recv,
     dots_send,
     dots_recv,
+    told,
     cam_jac,
     point_jac,
     obs_point,
@@ -141,15 +141,36 @@
 
     barrier = pltpu.get_barrier_semaphore()
 
-    def greet(offset, carry):
-        pl.semaphore_signal(
-            barrier, inc=1, device_id=(lax.rem(me + offset, n),), device_id_type=MESH
-        )
-        return carry
-
     from_prev[...] = jnp.zeros_like(from_prev)
     from_next[...] = jnp.zeros_like(from_next)
-    lax.fori_loop(1, n, greet, 0)
+
+    reaches = []
+    while 2 ** len(reaches) < n:
+        reaches.insert(0, 2 ** len(reaches))
+    has_next = me < n - 1
+    has_prev = me > 0
+    for reach in reaches:
+        pl.semaphore_signal(
+            barrier, inc=1, device_id=(lax.rem(me + n - reach, n),), device_id_type=MESH
+        )
+
+    @pl.when(has_next)
+    def _():
+        pl.semaphore_signal(barrier, inc=1, device_id=(me + 1,), device_id_type=MESH)
+
+    def tell(turn):
+        pl.semaphore_signal(
+            told.at[turn],
+            inc=1,
+            device_id=(lax.rem(me + reaches[turn], n),),
+            device_id_type=MESH,
+        )
+
+    def hear(turn):
+        pl.semaphore_wait(told.at[turn], 1)
+        if turn + 1 < len(reaches):
+            tell(turn + 1)
+
 
     loads["back_list"].wait()
     loads["front_list"].wait()
@@ -225,7 +246,12 @@
             group_of[spot] = jnp.where(used[spot], lax.shift_right_logical(side, 8), -1)
             lane_of[spot] = side & (WIDE - 1)
 
-    wide_row = iota((WIDE, slots), 0)
+    pair_rows = [
+        (iota((2 * GROUP, slots), 0) + first).astype(jnp.int16)
+        for first in range(0, WIDE, 2 * GROUP)
+    ]
+    unit = jnp.ones((2 * GROUP, slots), BF16)
+    nil = jnp.zeros((2 * GROUP, slots), BF16)
     group_row = iota((GROUP, slots), 0)
 
     def scatter(source, count, cam):
@@ -234,7 +260,10 @@
             jnp.where(mask, jnp.broadcast_to(source[index, cam : cam + 1], (GROUP, slots)), 0.0)
             for index in range(SPLITS * count)
         ]
-        hot = jnp.where(wide_row == lane_of[cam : cam + 1], 1.0, 0.0).astype(BF16)
+        lanes = jnp.broadcast_to(lane_of[cam : cam + 1], (2 * GROUP, slots)).astype(jnp.int16)
+        hot = jnp.concatenate(
+            [jnp.where(row == lanes, unit, nil) for row in pair_rows], axis=0
+        )
         return dot_nt(jnp.concatenate(blocks, axis=0).astype(BF16), hot)
 
     def joined(sums, index):
@@ -264,9 +293,6 @@
             device_id_type=MESH,
         )
 
-    has_next = me < n - 1
-    has_prev = me > 0
-
     def send(sums, turn):
         spot = FIRST_ROWS[turn]
         for index, member in enumerate(sums):
@@ -418,10 +444,13 @@
     for index, block in enumerate(blocks):
         for step, term in enumerate(splits_of(block)):
             first_terms[SPLITS * index + step] = term
-    whole = scatter(first_terms, 9, 0)
-    for cam in range(1, cams):
-        whole = whole + scatter(first_terms, 9, cam)
-    sums = [joined(whole, index) for index in range(9)]
+    chains = [scatter(first_terms, 9, 0), scatter(first_terms, 9, 1)]
+    for cam in range(2, cams):
+        chains[cam % 2] = chains[cam % 2] + scatter(first_terms, 9, cam)
+    for index in range(9):
+        coupling[index] = joined(chains[0], index)
+    whole = chains[1]
+    sums = [joined(whole, index) + coupling[index] for index in range(9)]
 
     damping = jnp.zeros((SPLITS * GROUP, WIDE), F32)
     damp_row = iota((GROUP, WIDE), 0)
@@ -441,7 +470,8 @@
         if lead == tail:
             sums[index] = sums[index] + moved
 
-    pl.semaphore_wait(barrier, n - 1)
+    pl.semaphore_wait(barrier, len(reaches) + jnp.where(has_prev, 1, 0))
+    tell(0)
     send(sums, 0)
 
     for top in range(0, cams, GROUP):
@@ -477,6 +507,7 @@
         squares[index] = spread_out(total)
     image = square_product(start)
 
+    hear(0)
     sums = receive(sums, 0)
     inverse = symmetric_inverse(sums[:6])
     back = camera_product(apply_inverse(inverse, sums[6:]))
@@ -485,7 +516,9 @@
 
     sums = point_product(direction)
     send(sums, 1)
+    hear(1)
     square_direction = square_product(direction)
+    hear(2)
     sums = receive(sums, 1)
     values = apply_inverse(inverse, sums)
     back = camera_product(values)
@@ -494,6 +527,7 @@
 
     sums_ahead = point_product(ahead)
     send(sums_ahead, 2)
+    hear(3)
     square_ahead = square_product(ahead)
     inner = dot_of(residual, direction)
     curve = dot_of(direction, image)
@@ -519,6 +553,8 @@
     for index, member in enumerate(members):
         packed = jnp.where(dot_lane == index, member, packed)
     dots_out[1] = shift
+    for turn in range(4, len(reaches)):
+        hear(turn)
     sums_ahead = receive(sums_ahead, 2)
     values_ahead = apply_inverse(inverse, sums_ahead)
     wide_shift = jnp.concatenate([shift] * halves, axis=1)
@@ -568,8 +604,8 @@
         seen = image[entry] - step * further[entry] + ratio * image[entry]
         solved = start[entry] + step * direction[entry] + second * fresh
         left = residual[entry] - step * image[entry] - second * seen
-        step_out[entry : entry + 1] = line(solved)
-        residual_out[entry : entry + 1] = line(left)
+        packed_out[entry : entry + 1] = line(solved)
+        packed_out[16 + entry : 17 + entry] = line(left)
 
 
 def solution(mesh):
@@ -601,11 +637,11 @@
             start_guess,
         )
         vector = jax.ShapeDtypeStruct(right_side.shape, F32)
-        return pl.pallas_call(
+        found = pl.pallas_call(
             functools.partial(kernel, n),
-            out_shape=(vector, vector),
+            out_shape=pltpu.VMEM((32, right_side.shape[1]), F32),
             in_specs=[pl.BlockSpec(memory_space=pltpu.HBM)] * 10,
-            out_specs=(pl.BlockSpec(memory_space=pltpu.VMEM),) * 2,
+            out_specs=pl.BlockSpec(memory_space=pltpu.VMEM),
             scratch_shapes=[
                 pltpu.VMEM((cams, slots), I32),
                 pltpu.VMEM((cams, slots), I32),
@@ -628,6 +664,7 @@
                 pltpu.SemaphoreType.DMA((3,)),
                 pltpu.SemaphoreType.DMA,
                 pltpu.SemaphoreType.DMA,
+                pltpu.SemaphoreType.REGULAR((max(1, (n - 1).bit_length()),)),
                 *[pltpu.VMEM(member.shape, member.dtype) for member in operands],
                 pltpu.SemaphoreType.DMA((len(operands),)),
             ],
@@ -636,6 +673,7 @@
             ),
             name="schur_cg",
         )(*operands)
+        return found[:9], found[16:25]
 
     return jax.shard_map(
         shards,

time: 25.3 us -> 22.7 us (0.90)
  Pallas kernels: 22.6 us -> 21.3 us
  local copies, waits for them, and re-layouts: 1.9 us -> 0.61 us
    unnamed x4 -> x0, local copies, waits for them, and re-layouts: 1.9 us -> none
    pallas_call x1, Pallas kernels: 22.6 us -> 21.3 us  [shards(): pl.pallas_call(functools.partial(kernel, n), out_shape=pltpu.VMEM((32, ri...]
    slice x0 -> x1, local copies, waits for them, and re-layouts: none -> 0.61 us  [shards(): return (found[:9], found[16:25])]
where the time goes in v2:
time: 22.7 us; the launch traced here: 22.5 us
  Pallas kernels  21.3 us (94%)
  between operations  0.64 us (3%)
  local copies, waits for them, and re-layouts  0.61 us (3%)
    pallas_call x1, Pallas kernels, shards(): pl.pallas_call(functools.partial(kernel, n), out_shape=pltpu.VMEM((32, ri...  21.3 us
    slice x1, local copies, waits for them, and re-layouts, shards(): return (found[:9], found[16:25])  0.61 us

profile of v2, /device:TPU:0, one launch (start us, length us, event | category | flops | bytes accessed | tf_op | source)
XLA Modules:
  0.0 22.5 jit_solution(5384175714691861040)
XLA Ops:
  0.6 21.3 %schur_cg.1 = f32[32,16]{1,0:T(8,128)S(1)} custom-call(bf16[18,16,512]{2,1,0:T(8,128)(2,1)} %cam_jac_hbm.1, bf16[6,16,512]{2,1,0:T(8,128)(2,1)} %point_jac_hbm.1, s32[16,512]{1,0:T(8,128)} %obs_point_hbm.1, s32[1,16]{1,0:T(1,128)} %bitcast.4, s32[1,384]{1,0:T(1,128)} %back_list_hbm.1, s32[1,384]{1,0:T(1,128)} %front_list_hbm.1, f32[1,1024]{1,0:T(1,128)} %bitcast.3, ...), custom_call_target="tpu_custom_call" | custom-call | tf_op jit(solution)/shard_map/schur_cg/pallas_call | solution.py:640
  21.9 0.6 %fusion = (f32[9,16]{1,0:T(8,128)}, f32[9,16]{1,0:T(8,128)}) fusion(f32[32,16]{1,0:T(8,128)S(1)} %schur_cg.1), kind=kLoop, calls=%fused_computation | loop fusion | bytes 2304 | tf_op jit(solution)/shard_map/slice | solution.py:676

commit v3 on v2

--- a/solution.py
+++ b/solution.py
@@ -17,16 +17,16 @@
 FIRST_ROWS = (0, 9, 12)
 SQUARES = tuple((lead, tail) for lead in range(9) for tail in range(lead, 9))
 LOAD_ORDER = (
+    "obs_count",
+    "obs_point",
+    "start_guess",
+    "point_jac",
+    "cam_jac",
     "back_list",
     "front_list",
-    "obs_count",
-    "obs_point",
+    "point_damp",
     "cam_damp",
-    "start_guess",
     "right_side",
-    "point_damp",
-    "point_jac",
-    "cam_jac",
 )
 
 
@@ -120,7 +120,6 @@
     points = point_damp.shape[1]
     border = back_list.shape[1]
     edge = border // LANES
-    own_groups = points // WIDE
     halves = WIDE // LANES
     me = lax.axis_index("seg")
 
@@ -172,37 +171,6 @@
             tell(turn + 1)
 
 
-    loads["back_list"].wait()
-    loads["front_list"].wait()
-    listed = jnp.concatenate([back_list[...], front_list[...]], axis=1)
-    total = 2 * border
-    place = iota((1, total), 1)
-    in_front = place >= border
-    place = jnp.where(in_front, place - border, place)
-    list_group = jnp.where(in_front, edge, 0) + lax.shift_right_logical(place, 7)
-    list_lane = jnp.where(in_front, LANES, 0) + (place & (LANES - 1))
-    row = iota((2 * own_groups, total), 0)
-    code = jnp.where(row < own_groups, list_group + 1, list_lane)
-    wanted = jnp.where(row < own_groups, row, row - own_groups)
-    code = jnp.where(lax.shift_right_logical(listed, 8) == wanted, code, 0)
-    hot = jnp.where(iota((WIDE, total), 0) == (listed & (WIDE - 1)), 1.0, 0.0).astype(BF16)
-    table = dot_nt(code.astype(F32).astype(BF16), hot)
-    table_group = table[:own_groups]
-    table_lane = table[own_groups:]
-    other = jnp.where(table_group == 0.0, 1.0, 0.0)
-    before = jnp.where(iota((WIDE, WIDE), 0) < iota((WIDE, WIDE), 1), 1.0, 0.0).astype(BF16)
-    rank = jnp.dot(other.astype(BF16), before, preferred_element_type=F32)
-    counts = jnp.sum(other, axis=1, keepdims=True)
-    table_row = iota((own_groups, WIDE), 0)
-    for index in range(own_groups - 1):
-        rank = rank + jnp.where(table_row > index, counts[index : index + 1], 0.0)
-    rank = rank.astype(I32)
-    is_other = other > 0.0
-    table_group = jnp.where(
-        is_other, (2 * edge + lax.shift_right_logical(rank, 8)).astype(F32), table_group - 1.0
-    )
-    table_lane = jnp.where(is_other, (rank & (WIDE - 1)).astype(F32), table_lane)
-
     eye = iota((cams, cams), 0) == iota((cams, cams), 1)
 
     def column(line):
@@ -217,35 +185,16 @@
     used_count = column(obs_count[...].astype(F32)).astype(I32)
     used = iota((cams, slots), 1) < used_count
 
-    code_table = (table_group * WIDE + table_lane).astype(I32)
-    rows_of_table = [
-        jnp.broadcast_to(
-            code_table[index // halves : index // halves + 1, part * LANES : (part + 1) * LANES],
-            (GROUP, LANES),
-        )
-        for index in range(own_groups * halves)
-        for part in (index % halves,)
+    ids = obs_point[...]
+    group_of[...] = jnp.where(used, lax.shift_right_logical(ids, 7) & (GROUP - 1), -1)
+    lane_of[...] = (ids & (LANES - 1)) + jnp.where(ids < points, 0, LANES)
+
+    columns = jnp.transpose(lane_of[...].astype(F32)).astype(I32)
+    lane_numbers = [
+        (iota((slots, LANES), 1) + part * LANES).astype(jnp.int16) for part in range(halves)
     ]
-    for top in range(0, cams, GROUP):
-        for left in range(0, slots, LANES):
-            spot = (slice(top, top + GROUP), slice(left, left + LANES))
-            ids = obs_point[spot]
-            back_slot = ids - points
-            front_slot = back_slot - border
-            in_back = ids < points + border
-            side = jnp.where(
-                in_back,
-                lax.shift_right_logical(back_slot, 7) * WIDE + LANES + (back_slot & (LANES - 1)),
-                (edge + lax.shift_right_logical(front_slot, 7)) * WIDE + (front_slot & (LANES - 1)),
-            )
-            id_row = lax.shift_right_logical(ids, 7)
-            id_lane = ids & (LANES - 1)
-            for index, row in enumerate(rows_of_table):
-                found = jnp.take_along_axis(row, id_lane, axis=1, mode="promise_in_bounds")
-                side = jnp.where(id_row == index, found, side)
-            group_of[spot] = jnp.where(used[spot], lax.shift_right_logical(side, 8), -1)
-            lane_of[spot] = side & (WIDE - 1)
-
+    tall_unit = jnp.ones((slots, LANES), BF16)
+    tall_nil = jnp.zeros((slots, LANES), BF16)
     pair_rows = [
         (iota((2 * GROUP, slots), 0) + first).astype(jnp.int16)
         for first in range(0, WIDE, 2 * GROUP)
@@ -265,6 +214,22 @@
             [jnp.where(row == lanes, unit, nil) for row in pair_rows], axis=0
         )
         return dot_nt(jnp.concatenate(blocks, axis=0).astype(BF16), hot)
+
+    def first_scatter(cam):
+        mask = group_row == group_of[cam : cam + 1]
+        blocks = [
+            jnp.where(
+                mask, jnp.broadcast_to(first_terms[index, cam : cam + 1], (GROUP, slots)), 0.0
+            )
+            for index in range(SPLITS * 9)
+        ]
+        wide = jnp.broadcast_to(columns[:, cam : cam + 1], (slots, LANES)).astype(jnp.int16)
+        hot = [jnp.where(lanes == wide, tall_unit, tall_nil) for lanes in lane_numbers]
+        return jnp.dot(
+            jnp.concatenate(blocks, axis=0).astype(BF16),
+            jnp.concatenate(hot, axis=1),
+            preferred_element_type=F32,
+        )
 
     def joined(sums, index):
         whole = sums[(SPLITS * index + SPLITS - 1) * GROUP : (SPLITS * index + SPLITS) * GROUP]
@@ -293,19 +258,31 @@
             device_id_type=MESH,
         )
 
+    row_of = iota((GROUP, LANES), 0)
+    low_row = row_of < edge
+
+    def looked_up(tile, rows, tile_row, tile_lane, start):
+        for row in range(rows):
+            wide = jnp.broadcast_to(tile[row : row + 1], tile_lane.shape)
+            found = jnp.take_along_axis(wide, tile_lane, axis=1, mode="promise_in_bounds")
+            start = jnp.where(tile_row == row, found, start)
+        return start
+
+    def start_pair(turn, size):
+        @pl.when(has_next)
+        def _():
+            neighbour("next", turn, size).start()
+
+        @pl.when(has_prev)
+        def _():
+            neighbour("prev", turn, size).start()
+
     def send(sums, turn):
         spot = FIRST_ROWS[turn]
         for index, member in enumerate(sums):
             to_next[spot + index] = member[:, :LANES]
             to_prev[spot + index] = member[:, LANES:]
-
-        @pl.when(has_next)
-        def _():
-            neighbour("next", turn, len(sums)).start()
-
-        @pl.when(has_prev)
-        def _():
-            neighbour("prev", turn, len(sums)).start()
+        start_pair(turn, len(sums))
 
     edge_row = iota((GROUP, LANES), 0) < 2 * edge
 
@@ -420,20 +397,24 @@
         dots_copy(offset).start()
         return carry
 
-    for name in LOAD_ORDER[4:]:
+    for name in LOAD_ORDER[2:]:
         loads[name].wait()
-    damp = column(cam_damp[...])
     start_col = [column(start_guess[entry : entry + 1]) for entry in range(9)]
-    right = [spread_out(column(right_side[entry : entry + 1])) for entry in range(9)]
-    start = [spread_out(member) for member in start_col]
-
-    for index in range(18):
-        wide_jac[index] = jnp.where(used, cam_jac[index].astype(F32), 0.0)
+    listed = [back_list, front_list]
+    listed = [
+        member[:, part * LANES : (part + 1) * LANES] for member in listed for part in range(edge)
+    ]
+    listed = jnp.concatenate(
+        listed + [jnp.full((GROUP - 2 * edge, LANES), -1, I32)], axis=0
+    )
+    list_row = lax.shift_right_arithmetic(listed, 7)
+    list_lane = listed & (LANES - 1)
+
     errors = []
     for side in range(2):
-        running = wide_jac[9 * side] * start_col[0]
+        running = cam_jac[9 * side].astype(F32) * start_col[0]
         for entry in range(1, 9):
-            running = running + wide_jac[9 * side + entry] * start_col[entry]
+            running = running + cam_jac[9 * side + entry].astype(F32) * start_col[entry]
         errors.append(running)
     blocks = [
         pjac(lead) * pjac(tail) + pjac(3 + lead) * pjac(3 + tail) for lead, tail in ENTRY_PAIRS
@@ -444,35 +425,109 @@
     for index, block in enumerate(blocks):
         for step, term in enumerate(splits_of(block)):
             first_terms[SPLITS * index + step] = term
-    chains = [scatter(first_terms, 9, 0), scatter(first_terms, 9, 1)]
-    for cam in range(2, cams):
-        chains[cam % 2] = chains[cam % 2] + scatter(first_terms, 9, cam)
+    chains = [None, None]
+    for cam in range(cams):
+        tall = cam % 2 == 0 or cam % 8 == 3
+        part = first_scatter(cam) if tall else scatter(first_terms, 9, cam)
+        before = chains[0 if tall else 1]
+        chains[0 if tall else 1] = part if before is None else before + part
     for index in range(9):
         coupling[index] = joined(chains[0], index)
     whole = chains[1]
     sums = [joined(whole, index) + coupling[index] for index in range(9)]
 
-    damping = jnp.zeros((SPLITS * GROUP, WIDE), F32)
-    damp_row = iota((GROUP, WIDE), 0)
-    square_row = iota((WIDE, WIDE), 0)
-    for index in range(own_groups):
-        here = point_damp[:, index * WIDE : (index + 1) * WIDE]
-        mask = damp_row == table_group[index : index + 1].astype(I32)
-        block = jnp.concatenate([jnp.where(mask, term, 0.0) for term in splits_of(here)], axis=0)
-        hot = jnp.where(
-            square_row == table_lane[index : index + 1].astype(I32), 1.0, 0.0
-        ).astype(BF16)
-        damping = damping + dot_nt(block.astype(BF16), hot)
-    moved = damping[(SPLITS - 1) * GROUP :]
-    for step in reversed(range(SPLITS - 1)):
-        moved = moved + damping[step * GROUP : (step + 1) * GROUP]
-    for index, (lead, tail) in enumerate(ENTRY_PAIRS):
-        if lead == tail:
-            sums[index] = sums[index] + moved
+    moved = [point_damp[:, part * LANES : (part + 1) * LANES] for part in range(GROUP)]
+    moved = jnp.concatenate(moved, axis=0)
+    tiles = []
+    for index, (member, pair) in enumerate(zip(sums, ENTRY_PAIRS + ((0, 1),) * 3)):
+        own, side = member[:, :LANES], member[:, LANES:]
+        if pair[0] == pair[1]:
+            own = own + moved
+        chosen = looked_up(own, GROUP, list_row, list_lane, jnp.zeros((GROUP, LANES), F32))
+        tiles.append(
+            (own, jnp.where(low_row, chosen, side), jnp.where(low_row, side, chosen))
+        )
+        to_next[index], to_prev[index] = tiles[-1][1], tiles[-1][2]
 
     pl.semaphore_wait(barrier, len(reaches) + jnp.where(has_prev, 1, 0))
     tell(0)
-    send(sums, 0)
+    start_pair(0, 9)
+
+    for index in range(18):
+        wide_jac[index] = jnp.where(used, cam_jac[index].astype(F32), 0.0)
+    damp = column(cam_damp[...])
+    right = [spread_out(column(right_side[entry : entry + 1])) for entry in range(9)]
+    start = [spread_out(member) for member in start_col]
+
+    flat = jnp.concatenate([back_list[...], front_list[...]], axis=1)
+    place = iota((1, 2 * border), 1)
+    code_row = iota((2 * GROUP, 2 * border), 0)
+    code = jnp.where(
+        code_row < GROUP, lax.shift_right_logical(place, 7) + 1, place & (LANES - 1)
+    )
+    code = jnp.where(lax.shift_right_logical(flat, 7) == (code_row & (GROUP - 1)), code, 0)
+    hot = jnp.where(iota((LANES, 2 * border), 0) == (flat & (LANES - 1)), 1.0, 0.0).astype(BF16)
+    table = dot_nt(code.astype(F32).astype(BF16), hot).astype(I32)
+    place_row = table[:GROUP] - 1
+    place_lane = table[GROUP:]
+    other = place_row < 0
+    count = jnp.where(other, 1.0, 0.0)
+    before = jnp.where(iota((LANES, LANES), 0) < iota((LANES, LANES), 1), 1.0, 0.0).astype(BF16)
+    double = jnp.concatenate([count, jnp.zeros((GROUP, LANES), F32)], axis=0).astype(BF16)
+    rank = jnp.dot(double, before, preferred_element_type=F32)[:GROUP]
+    total = jnp.sum(count, axis=1, keepdims=True)
+    for row in range(GROUP - 1):
+        rank = rank + jnp.where(row_of > row, total[row : row + 1], 0.0)
+    rank = rank.astype(I32)
+    code_table = jnp.where(
+        other,
+        2 * edge * WIDE + rank,
+        place_row * WIDE + place_lane + jnp.where(place_row < edge, 0, LANES),
+    )
+    aim = jnp.where(other, rank, -1)
+    slot_row = iota((WIDE, LANES), 0)
+    hot = [jnp.where(slot_row == aim[row : row + 1], 1.0, 0.0) for row in range(GROUP)]
+    hot = jnp.concatenate(hot, axis=1).astype(BF16)
+    code_row = iota((2 * GROUP, points), 0)
+    place = iota((2 * GROUP, points), 1)
+    code = jnp.where(
+        code_row < GROUP, lax.shift_right_logical(place, 7) + 1, place & (LANES - 1)
+    )
+    table = dot_nt(code.astype(F32).astype(BF16), hot).astype(I32)
+
+    def in_place(line):
+        return jnp.where(
+            row_of == 2 * edge,
+            jnp.broadcast_to(line[:, :LANES], (GROUP, LANES)),
+            jnp.broadcast_to(line[:, LANES:], (GROUP, LANES)),
+        )
+
+    rest_row = jnp.where(row_of < 2 * edge, -1, in_place(table[:1] - 1))
+    rest_lane = jnp.where(row_of < 2 * edge, 0, in_place(table[GROUP : GROUP + 1]))
+    sums = []
+    for own, left, right_half in tiles:
+        rest = looked_up(own, GROUP, rest_row, rest_lane, jnp.zeros((GROUP, LANES), F32))
+        left = left + jnp.where(row_of == 2 * edge, rest, 0.0)
+        moved = pltpu.roll(rest, GROUP - 1, 0)
+        right_half = right_half + jnp.where(row_of == 2 * edge, moved, 0.0)
+        sums.append(jnp.concatenate([left, right_half], axis=1))
+
+    for top in range(0, cams, GROUP):
+        for left in range(0, slots, LANES):
+            spot = (slice(top, top + GROUP), slice(left, left + LANES))
+            ids = obs_point[spot]
+            back_slot = ids - points
+            front_slot = back_slot - border
+            in_back = ids < points + border
+            side = jnp.where(
+                in_back,
+                lax.shift_right_logical(back_slot, 7) * WIDE + LANES + (back_slot & (LANES - 1)),
+                (edge + lax.shift_right_logical(front_slot, 7)) * WIDE + (front_slot & (LANES - 1)),
+            )
+            id_row = lax.shift_right_logical(ids, 7)
+            side = looked_up(code_table, GROUP, id_row, ids & (LANES - 1), side)
+            group_of[spot] = jnp.where(used[spot], lax.shift_right_logical(side, 8), -1)
+            lane_of[spot] = side & (WIDE - 1)
 
     for top in range(0, cams, GROUP):
         for left in range(0, slots, LANES):

time: 22.7 us -> 21.8 us (0.960)
  Pallas kernels: 21.3 us -> 20.4 us
    pallas_call x1, Pallas kernels: 21.3 us -> 20.4 us  [shards(): pl.pallas_call(functools.partial(kernel, n), out_shape=pltpu.VMEM((32, ri...]
where the time goes in v3:
time: 21.8 us; the launch traced here: 21.7 us
  Pallas kernels  20.4 us (94%)
  between operations  0.64 us (3%)
  local copies, waits for them, and re-layouts  0.61 us (3%)
    pallas_call x1, Pallas kernels, shards(): pl.pallas_call(functools.partial(kernel, n), out_shape=pltpu.VMEM((32, ri...  20.4 us
    slice x1, local copies, waits for them, and re-layouts, shards(): return (found[:9], found[16:25])  0.61 us

profile of v3, /device:TPU:0, one launch (start us, length us, event | category | flops | bytes accessed | tf_op | source)
XLA Modules:
  0.0 21.7 jit_solution(2402430655111629266)
XLA Ops:
  0.6 20.4 %schur_cg.1 = f32[32,16]{1,0:T(8,128)S(1)} custom-call(bf16[18,16,512]{2,1,0:T(8,128)(2,1)} %cam_jac_hbm.1, bf16[6,16,512]{2,1,0:T(8,128)(2,1)} %point_jac_hbm.1, s32[16,512]{1,0:T(8,128)} %obs_point_hbm.1, s32[1,16]{1,0:T(1,128)} %bitcast.4, s32[1,384]{1,0:T(1,128)} %back_list_hbm.1, s32[1,384]{1,0:T(1,128)} %front_list_hbm.1, f32[1,1024]{1,0:T(1,128)} %bitcast.3, ...), custom_call_target="tpu_custom_call" | custom-call | tf_op jit(solution)/shard_map/schur_cg/pallas_call | solution.py:695
  21.1 0.6 %fusion = (f32[9,16]{1,0:T(8,128)}, f32[9,16]{1,0:T(8,128)}) fusion(f32[32,16]{1,0:T(8,128)S(1)} %schur_cg.1), kind=kLoop, calls=%fused_computation | loop fusion | bytes 2304 | tf_op jit(solution)/shard_map/slice | solution.py:731

commit v4 on v3

--- a/solution.py
+++ b/solution.py
@@ -14,7 +14,7 @@
 WIDE = 256
 GROUP = 8
 SPLITS = 2
-FIRST_ROWS = (0, 9, 12)
+SIZES = (9, 3, 3)
 SQUARES = tuple((lead, tail) for lead in range(9) for tail in range(lead, 9))
 LOAD_ORDER = (
     "obs_count",
@@ -140,8 +140,15 @@
 
     barrier = pltpu.get_barrier_semaphore()
 
-    from_prev[...] = jnp.zeros_like(from_prev)
-    from_next[...] = jnp.zeros_like(from_next)
+    kept = 2 * edge
+    heights = (kept, GROUP, GROUP)
+    lengths = [-(-count * height // GROUP) * GROUP for count, height in zip(SIZES, heights)]
+    spots = [sum(lengths[:turn]) for turn in range(3)]
+
+    for landing in (from_prev, from_next):
+        landing[...] = jnp.zeros_like(landing)
+    for leaving in (to_next, to_prev):
+        leaving[lengths[0] - GROUP : lengths[0]] = jnp.zeros((GROUP, LANES), F32)
 
     reaches = []
     while 2 ** len(reaches) < n:
@@ -182,6 +189,8 @@
 
     loads["obs_count"].wait()
     loads["obs_point"].wait()
+    loads["start_guess"].wait()
+    start_col = [column(start_guess[entry : entry + 1]) for entry in range(9)]
     used_count = column(obs_count[...].astype(F32)).astype(I32)
     used = iota((cams, slots), 1) < used_count
 
@@ -238,8 +247,8 @@
             whole = whole + sums[first : first + GROUP]
         return whole
 
-    def neighbour(where, turn, size):
-        spot = FIRST_ROWS[turn]
+    def neighbour(where, turn):
+        spot, size = spots[turn], lengths[turn]
         if where == "next":
             return pltpu.make_async_remote_copy(
                 src_ref=to_next.at[pl.ds(spot, size)],
@@ -268,48 +277,45 @@
             start = jnp.where(tile_row == row, found, start)
         return start
 
-    def start_pair(turn, size):
+    def start_pair(turn):
         @pl.when(has_next)
         def _():
-            neighbour("next", turn, size).start()
+            neighbour("next", turn).start()
 
         @pl.when(has_prev)
         def _():
-            neighbour("prev", turn, size).start()
+            neighbour("prev", turn).start()
 
     def send(sums, turn):
-        spot = FIRST_ROWS[turn]
         for index, member in enumerate(sums):
-            to_next[spot + index] = member[:, :LANES]
-            to_prev[spot + index] = member[:, LANES:]
-        start_pair(turn, len(sums))
+            spot = spots[turn] + index * GROUP
+            to_next[spot : spot + GROUP] = member[:, :LANES]
+            to_prev[spot : spot + GROUP] = member[:, LANES:]
+        start_pair(turn)
 
     edge_row = iota((GROUP, LANES), 0) < 2 * edge
 
     def receive(sums, turn):
-        spot = FIRST_ROWS[turn]
         @pl.when(has_next)
         def _():
-            copy = neighbour("next", turn, len(sums))
+            copy = neighbour("next", turn)
             copy.wait_send()
-            neighbour("prev", turn, len(sums)).wait_recv()
+            neighbour("prev", turn).wait_recv()
 
         @pl.when(has_prev)
         def _():
-            copy = neighbour("prev", turn, len(sums))
+            copy = neighbour("prev", turn)
             copy.wait_send()
-            neighbour("next", turn, len(sums)).wait_recv()
-
-        return [
-            jnp.concatenate(
-                [
-                    member[:, :LANES] + jnp.where(edge_row, from_next[spot + index], 0.0),
-                    member[:, LANES:] + jnp.where(edge_row, from_prev[spot + index], 0.0),
-                ],
-                axis=1,
-            )
-            for index, member in enumerate(sums)
-        ]
+            neighbour("next", turn).wait_recv()
+
+        whole = []
+        for index, member in enumerate(sums):
+            spot = spots[turn] + index * heights[turn]
+            rows = slice(spot, spot + GROUP)
+            left = member[:, :LANES] + jnp.where(edge_row, from_next[rows], 0.0)
+            below = member[:, LANES:] + jnp.where(edge_row, from_prev[rows], 0.0)
+            whole.append(jnp.concatenate([left, below], axis=1))
+        return whole
 
     def pjac(index):
         return point_jac[index].astype(F32)
@@ -317,40 +323,38 @@
     def spread_out(col):
         return jnp.broadcast_to(col, (cams, LANES))
 
-    def point_product(vector):
+    def point_terms(running, entry, vector):
+        vector_rows[entry] = vector
+        for cam in range(cams):
+            scale = jnp.broadcast_to(vector_rows[entry, cam : cam + 1], (GROUP, LANES))
+            for index in range(3):
+                for part in range(halves):
+                    block = coupling[
+                        cam * 27 + index * 9 + entry, :, part * LANES : (part + 1) * LANES
+                    ]
+                    term = block * scale
+                    before = running[index][part]
+                    running[index][part] = term if before is None else before + term
+
+    def camera_entry(values, entry):
+        for cam in range(cams):
+            whole = None
+            for index in range(3):
+                for part in range(halves):
+                    lanes = slice(part * LANES, (part + 1) * LANES)
+                    term = coupling[cam * 27 + index * 9 + entry, :, lanes] * values[index][:, lanes]
+                    whole = term if whole is None else whole + term
+            partial[entry, cam * GROUP : (cam + 1) * GROUP] = whole
+        whole = partial[entry, pl.ds(0, cams, stride=GROUP)]
+        for row in range(1, GROUP):
+            whole = whole + partial[entry, pl.ds(row, cams, stride=GROUP)]
+        return spread_out(jnp.sum(whole, axis=1, keepdims=True))
+
+    def there_and_back(values, use):
+        running = [[None] * halves for index in range(3)]
         for entry in range(9):
-            vector_rows[entry] = vector[entry]
-        running = [[None] * halves for index in range(3)]
-        for cam in range(cams):
-            for entry in range(9):
-                scale = jnp.broadcast_to(vector_rows[entry, cam : cam + 1], (GROUP, LANES))
-                for index in range(3):
-                    for part in range(halves):
-                        block = coupling[
-                            cam * 27 + index * 9 + entry, :, part * LANES : (part + 1) * LANES
-                        ]
-                        term = block * scale
-                        before = running[index][part]
-                        running[index][part] = term if before is None else before + term
+            point_terms(running, entry, use(entry, camera_entry(values, entry)))
         return [jnp.concatenate(parts, axis=1) for parts in running]
-
-    def camera_product(values):
-        for cam in range(cams):
-            for entry in range(9):
-                whole = None
-                for index in range(3):
-                    for part in range(halves):
-                        lanes = slice(part * LANES, (part + 1) * LANES)
-                        term = coupling[cam * 27 + index * 9 + entry, :, lanes] * values[index][:, lanes]
-                        whole = term if whole is None else whole + term
-                partial[entry, cam * GROUP : (cam + 1) * GROUP] = whole
-        result = []
-        for entry in range(9):
-            whole = partial[entry, pl.ds(0, cams, stride=GROUP)]
-            for row in range(1, GROUP):
-                whole = whole + partial[entry, pl.ds(row, cams, stride=GROUP)]
-            result.append(spread_out(jnp.sum(whole, axis=1, keepdims=True)))
-        return result
 
     def square_product(vector):
         result = [None] * 9
@@ -397,9 +401,8 @@
         dots_copy(offset).start()
         return carry
 
-    for name in LOAD_ORDER[2:]:
+    for name in LOAD_ORDER[3:]:
         loads[name].wait()
-    start_col = [column(start_guess[entry : entry + 1]) for entry in range(9)]
     listed = [back_list, front_list]
     listed = [
         member[:, part * LANES : (part + 1) * LANES] for member in listed for part in range(edge)
@@ -410,27 +413,35 @@
     list_row = lax.shift_right_arithmetic(listed, 7)
     list_lane = listed & (LANES - 1)
 
-    errors = []
-    for side in range(2):
-        running = cam_jac[9 * side].astype(F32) * start_col[0]
-        for entry in range(1, 9):
-            running = running + cam_jac[9 * side + entry].astype(F32) * start_col[entry]
-        errors.append(running)
-    blocks = [
-        pjac(lead) * pjac(tail) + pjac(3 + lead) * pjac(3 + tail) for lead, tail in ENTRY_PAIRS
-    ]
-    blocks = blocks + [
-        errors[0] * pjac(entry) + errors[1] * pjac(3 + entry) for entry in range(3)
-    ]
-    for index, block in enumerate(blocks):
-        for step, term in enumerate(splits_of(block)):
-            first_terms[SPLITS * index + step] = term
     chains = [None, None]
-    for cam in range(cams):
-        tall = cam % 2 == 0 or cam % 8 == 3
-        part = first_scatter(cam) if tall else scatter(first_terms, 9, cam)
-        before = chains[0 if tall else 1]
-        chains[0 if tall else 1] = part if before is None else before + part
+    for top in range(0, cams, GROUP):
+        near = slice(top, top + GROUP)
+
+        def upper(ref, index):
+            return ref[index].astype(F32)[near]
+
+        errors = []
+        for side in range(2):
+            running = upper(cam_jac, 9 * side) * start_col[0][near]
+            for entry in range(1, 9):
+                running = running + upper(cam_jac, 9 * side + entry) * start_col[entry][near]
+            errors.append(running)
+        ours = [upper(point_jac, index) for index in range(6)]
+        blocks = [ours[lead] * ours[tail] + ours[3 + lead] * ours[3 + tail] for lead, tail in ENTRY_PAIRS]
+        blocks = blocks + [
+            errors[0] * ours[entry] + errors[1] * ours[3 + entry] for entry in range(3)
+        ]
+        for index, block in enumerate(blocks):
+            for step, term in enumerate(splits_of(block)):
+                first_terms[SPLITS * index + step, near] = term
+        for cam in range(top, top + GROUP):
+            side = 0 if cam % 2 == 0 or cam % 8 == 3 else 1
+            if side == 0 and cam not in (0, 2):
+                part = first_scatter(cam)
+            else:
+                part = scatter(first_terms, 9, cam)
+            before = chains[side]
+            chains[side] = part if before is None else before + part
     for index in range(9):
         coupling[index] = joined(chains[0], index)
     whole = chains[1]
@@ -447,11 +458,12 @@
         tiles.append(
             (own, jnp.where(low_row, chosen, side), jnp.where(low_row, side, chosen))
         )
-        to_next[index], to_prev[index] = tiles[-1][1], tiles[-1][2]
+        rows = slice(index * kept, (index + 1) * kept)
+        to_next[rows], to_prev[rows] = tiles[-1][1][:kept], tiles[-1][2][:kept]
 
     pl.semaphore_wait(barrier, len(reaches) + jnp.where(has_prev, 1, 0))
     tell(0)
-    start_pair(0, 9)
+    start_pair(0)
 
     for index in range(18):
         wide_jac[index] = jnp.where(used, cam_jac[index].astype(F32), 0.0)
@@ -560,27 +572,33 @@
             total = total + damp
             precond.append(spread_out(1.0 / total))
         squares[index] = spread_out(total)
-    image = square_product(start)
+    start_image = square_product(start)
 
     hear(0)
     sums = receive(sums, 0)
     inverse = symmetric_inverse(sums[:6])
-    back = camera_product(apply_inverse(inverse, sums[6:]))
-    residual = [right[entry] - (image[entry] - back[entry]) for entry in range(9)]
-    direction = [precond[entry] * residual[entry] for entry in range(9)]
-
-    sums = point_product(direction)
+    residual, direction = [], []
+
+    def first_use(entry, back):
+        residual.append(right[entry] - (start_image[entry] - back))
+        direction.append(precond[entry] * residual[entry])
+        return direction[entry]
+
+    sums = there_and_back(apply_inverse(inverse, sums[6:]), first_use)
     send(sums, 1)
     hear(1)
     square_direction = square_product(direction)
     hear(2)
     sums = receive(sums, 1)
     values = apply_inverse(inverse, sums)
-    back = camera_product(values)
-    image = [square_direction[entry] - back[entry] for entry in range(9)]
-    ahead = [precond[entry] * image[entry] for entry in range(9)]
-
-    sums_ahead = point_product(ahead)
+    image, ahead = [], []
+
+    def second_use(entry, back):
+        image.append(square_direction[entry] - back)
+        ahead.append(precond[entry] * image[entry])
+        return ahead[entry]
+
+    sums_ahead = there_and_back(values, second_use)
     send(sums_ahead, 2)
     hear(3)
     square_ahead = square_product(ahead)
@@ -621,19 +639,26 @@
     dots_out[0] = packed
     lax.fori_loop(1, n, start_dots, 0)
 
-    back = camera_product(values_ahead)
-    further = [square_ahead[entry] - back[entry] for entry in range(9)]
+    further = [square_ahead[entry] - camera_entry(values_ahead, entry) for entry in range(9)]
+
+    def lines(vector):
+        return jnp.concatenate([line(member) for member in vector], axis=0)
+
+    residual, direction, image, ahead, further = map(
+        lines, (residual, direction, image, ahead, further)
+    )
 
     pltpu.make_async_copy(dots_in, dots_in, dots_recv).wait()
     pltpu.make_async_copy(dots_in, dots_in, dots_send).wait()
 
-    def picked(row, low, high):
-        inside = (dot_lane >= low) & (dot_lane < high)
-        return jnp.sum(jnp.where(inside, row, 0.0), axis=1, keepdims=True)
+    def picked(row, lane):
+        wide = jnp.broadcast_to(row, (GROUP, LANES))
+        spot = jnp.full((GROUP, LANES), lane, I32)
+        return jnp.take_along_axis(wide, spot, axis=1, mode="promise_in_bounds")[:1]
 
     whole = packed + jnp.sum(dots_in[:, 0], axis=0)
-    inner = picked(whole, 0, 1)
-    curve = picked(whole, 1, 2)
+    inner = picked(whole, 0)
+    curve = picked(whole, 1)
     step = inner / curve
 
     def moved_by(row, about):
@@ -644,23 +669,17 @@
     whole = moved_by(packed, shift)
     for offset in range(1, n):
         whole = whole + moved_by(dots_in[offset - 1, 0], dots_in[offset - 1, 1])
-    one = (dot_lane == 2) | (dot_lane == 5) | (dot_lane == 8)
-    two = (dot_lane == 3) | (dot_lane == 6) | (dot_lane == 9)
-    three = (dot_lane == 4) | (dot_lane == 7)
-    inner_next = jnp.sum(jnp.where(one, whole, 0.0), axis=1, keepdims=True)
-    own_curve = jnp.sum(jnp.where(two, whole, 0.0), axis=1, keepdims=True)
-    cross = jnp.sum(jnp.where(three, whole, 0.0), axis=1, keepdims=True)
+    inner_next = picked(whole, 2) + picked(whole, 5) + picked(whole, 8)
+    own_curve = picked(whole, 3) + picked(whole, 6) + picked(whole, 9)
+    cross = picked(whole, 4) + picked(whole, 7)
     ratio = inner_next / inner
     curve = own_curve + ratio * (2.0 * cross + ratio * curve)
     second = inner_next / curve
-    for entry in range(9):
-        scaled = direction[entry] - step * ahead[entry]
-        fresh = scaled + ratio * direction[entry]
-        seen = image[entry] - step * further[entry] + ratio * image[entry]
-        solved = start[entry] + step * direction[entry] + second * fresh
-        left = residual[entry] - step * image[entry] - second * seen
-        packed_out[entry : entry + 1] = line(solved)
-        packed_out[16 + entry : 17 + entry] = line(left)
+    step, ratio, second = step[:, :cams], ratio[:, :cams], second[:, :cams]
+    fresh = direction - step * ahead + ratio * direction
+    seen = image - step * further + ratio * image
+    packed_out[:9] = start_guess[...] + step * direction + second * fresh
+    packed_out[16:25] = residual - step * image - second * seen
 
 
 def solution(mesh):
@@ -679,6 +698,8 @@
         start_guess,
     ):
         cams, slots = obs_point.shape
+        kept = 2 * (back_list.shape[1] // LANES)
+        link_rows = -(-SIZES[0] * kept // GROUP) * GROUP + sum(SIZES[1:]) * GROUP
         operands = (
             cam_jac,
             point_jac,
@@ -707,10 +728,10 @@
                 pltpu.VMEM((9, cams * GROUP, LANES), F32),
                 pltpu.VMEM((9, cams, LANES), F32),
                 pltpu.VMEM((len(SQUARES), cams, LANES), F32),
-                pltpu.VMEM((15, GROUP, LANES), F32),
-                pltpu.VMEM((15, GROUP, LANES), F32),
-                pltpu.VMEM((15, GROUP, LANES), F32),
-                pltpu.VMEM((15, GROUP, LANES), F32),
+                pltpu.VMEM((link_rows, LANES), F32),
+                pltpu.VMEM((link_rows, LANES), F32),
+                pltpu.VMEM((link_rows, LANES), F32),
+                pltpu.VMEM((link_rows, LANES), F32),
                 pltpu.VMEM((2, 1, LANES), F32),
                 pltpu.VMEM((n - 1, 2, 1, LANES), F32),
                 pltpu.SemaphoreType.DMA((3,)),

time: 21.8 us -> 21.7 us (level)
  no operation moved by 1% of the time
where the time goes in v4:
time: 21.7 us; the launch traced here: 21.6 us
  Pallas kernels  20.3 us (94%)
  between operations  0.64 us (3%)
  local copies, waits for them, and re-layouts  0.61 us (3%)
    pallas_call x1, Pallas kernels, shards(): pl.pallas_call(functools.partial(kernel, n), out_shape=pltpu.VMEM((32, ri...  20.3 us
    slice x1, local copies, waits for them, and re-layouts, shards(): return (found[:9], found[16:25])  0.61 us

profile of v4, /device:TPU:0, one launch (start us, length us, event | category | flops | bytes accessed | tf_op | source)
XLA Modules:
  0.0 21.6 jit_solution(13484377929486606573)
XLA Ops:
  0.6 20.3 %schur_cg.1 = f32[32,16]{1,0:T(8,128)S(1)} custom-call(bf16[18,16,512]{2,1,0:T(8,128)(2,1)} %cam_jac_hbm.1, bf16[6,16,512]{2,1,0:T(8,128)(2,1)} %point_jac_hbm.1, s32[16,512]{1,0:T(8,128)} %obs_point_hbm.1, s32[1,16]{1,0:T(1,128)} %bitcast.4, s32[1,384]{1,0:T(1,128)} %back_list_hbm.1, s32[1,384]{1,0:T(1,128)} %front_list_hbm.1, f32[1,1024]{1,0:T(1,128)} %bitcast.3, ...), custom_call_target="tpu_custom_call" | custom-call | tf_op jit(solution)/shard_map/schur_cg/pallas_call | solution.py:716
  21.0 0.6 %fusion = (f32[9,16]{1,0:T(8,128)}, f32[9,16]{1,0:T(8,128)}) fusion(f32[32,16]{1,0:T(8,128)S(1)} %schur_cg.1), kind=kLoop, calls=%fused_computation | loop fusion | bytes 2304 | tf_op jit(solution)/shard_map/slice | solution.py:752

commit v5 on v4

--- a/solution.py
+++ b/solution.py
@@ -91,10 +91,8 @@
     partial,
     vector_rows,
     squares,
-    to_next,
-    to_prev,
-    from_prev,
-    from_next,
+    leaving,
+    landing,
     dots_out,
     dots_in,
     next_send,
@@ -145,10 +143,9 @@
     lengths = [-(-count * height // GROUP) * GROUP for count, height in zip(SIZES, heights)]
     spots = [sum(lengths[:turn]) for turn in range(3)]
 
-    for landing in (from_prev, from_next):
-        landing[...] = jnp.zeros_like(landing)
-    for leaving in (to_next, to_prev):
-        leaving[lengths[0] - GROUP : lengths[0]] = jnp.zeros((GROUP, LANES), F32)
+    landing[...] = jnp.zeros_like(landing)
+    for side in range(2):
+        leaving[side, lengths[0] - GROUP : lengths[0]] = jnp.zeros((GROUP, LANES), F32)
 
     reaches = []
     while 2 ** len(reaches) < n:
@@ -251,16 +248,16 @@
         spot, size = spots[turn], lengths[turn]
         if where == "next":
             return pltpu.make_async_remote_copy(
-                src_ref=to_next.at[pl.ds(spot, size)],
-                dst_ref=from_prev.at[pl.ds(spot, size)],
+                src_ref=leaving.at[0, pl.ds(spot, size)],
+                dst_ref=landing.at[1, pl.ds(spot, size)],
                 send_sem=next_send.at[turn],
                 recv_sem=next_recv.at[turn],
                 device_id=(lax.rem(me + 1, n),),
                 device_id_type=MESH,
             )
         return pltpu.make_async_remote_copy(
-            src_ref=to_prev.at[pl.ds(spot, size)],
-            dst_ref=from_next.at[pl.ds(spot, size)],
+            src_ref=leaving.at[1, pl.ds(spot, size)],
+            dst_ref=landing.at[0, pl.ds(spot, size)],
             send_sem=prev_send.at[turn],
             recv_sem=prev_recv.at[turn],
             device_id=(lax.rem(me + n - 1, n),),
@@ -286,35 +283,39 @@
         def _():
             neighbour("prev", turn).start()
 
+    even = (me & 1) == 0
+    near = me & 1
+    far = 1 - near
+    edge_row = row_of < 2 * edge
+
     def send(sums, turn):
         for index, member in enumerate(sums):
-            spot = spots[turn] + index * GROUP
-            to_next[spot : spot + GROUP] = member[:, :LANES]
-            to_prev[spot : spot + GROUP] = member[:, LANES:]
+            rows = slice(spots[turn] + index * GROUP, spots[turn] + (index + 1) * GROUP)
+            leaving[near, rows] = member[0]
+            leaving[far, rows] = member[1]
         start_pair(turn)
 
-    edge_row = iota((GROUP, LANES), 0) < 2 * edge
-
-    def receive(sums, turn):
-        @pl.when(has_next)
+    def wait_next(turn, when):
+        @pl.when(jnp.logical_and(has_next, when))
         def _():
-            copy = neighbour("next", turn)
-            copy.wait_send()
+            neighbour("next", turn).wait_send()
             neighbour("prev", turn).wait_recv()
 
-        @pl.when(has_prev)
+    def wait_prev(turn, when):
+        @pl.when(jnp.logical_and(has_prev, when))
         def _():
-            copy = neighbour("prev", turn)
-            copy.wait_send()
+            neighbour("prev", turn).wait_send()
             neighbour("next", turn).wait_recv()
 
+    def arrived(sums, turn, side):
+        odd = jnp.logical_not(even)
+        wait_next(turn, odd if side else even)
+        wait_prev(turn, even if side else odd)
         whole = []
         for index, member in enumerate(sums):
             spot = spots[turn] + index * heights[turn]
-            rows = slice(spot, spot + GROUP)
-            left = member[:, :LANES] + jnp.where(edge_row, from_next[rows], 0.0)
-            below = member[:, LANES:] + jnp.where(edge_row, from_prev[rows], 0.0)
-            whole.append(jnp.concatenate([left, below], axis=1))
+            came = landing[(near, far)[side], spot : spot + GROUP]
+            whole.append(member[side] + jnp.where(edge_row, came, 0.0))
         return whole
 
     def pjac(index):
@@ -328,23 +329,26 @@
         for cam in range(cams):
             scale = jnp.broadcast_to(vector_rows[entry, cam : cam + 1], (GROUP, LANES))
             for index in range(3):
-                for part in range(halves):
-                    block = coupling[
-                        cam * 27 + index * 9 + entry, :, part * LANES : (part + 1) * LANES
-                    ]
-                    term = block * scale
-                    before = running[index][part]
-                    running[index][part] = term if before is None else before + term
+                for side, half in enumerate((near, far)):
+                    term = coupling[half, cam * 27 + index * 9 + entry] * scale
+                    before = running[index][side]
+                    running[index][side] = term if before is None else before + term
+
+    def near_products(values):
+        for entry in range(9):
+            for cam in range(cams):
+                whole = coupling[near, cam * 27 + entry] * values[0]
+                for index in range(1, 3):
+                    whole = whole + coupling[near, cam * 27 + index * 9 + entry] * values[index]
+                partial[entry, cam * GROUP : (cam + 1) * GROUP] = whole
 
     def camera_entry(values, entry):
         for cam in range(cams):
-            whole = None
+            rows = slice(cam * GROUP, (cam + 1) * GROUP)
+            whole = partial[entry, rows]
             for index in range(3):
-                for part in range(halves):
-                    lanes = slice(part * LANES, (part + 1) * LANES)
-                    term = coupling[cam * 27 + index * 9 + entry, :, lanes] * values[index][:, lanes]
-                    whole = term if whole is None else whole + term
-            partial[entry, cam * GROUP : (cam + 1) * GROUP] = whole
+                whole = whole + coupling[far, cam * 27 + index * 9 + entry] * values[index]
+            partial[entry, rows] = whole
         whole = partial[entry, pl.ds(0, cams, stride=GROUP)]
         for row in range(1, GROUP):
             whole = whole + partial[entry, pl.ds(row, cams, stride=GROUP)]
@@ -354,7 +358,7 @@
         running = [[None] * halves for index in range(3)]
         for entry in range(9):
             point_terms(running, entry, use(entry, camera_entry(values, entry)))
-        return [jnp.concatenate(parts, axis=1) for parts in running]
+        return running
 
     def square_product(vector):
         result = [None] * 9
@@ -372,19 +376,18 @@
         return jnp.sum(running, axis=0, keepdims=True)
 
     dot_lane = iota((1, LANES), 1)
-    part_row = iota((GROUP, WIDE), 0)
-    part_left = iota((GROUP, WIDE), 1) < LANES
-    own_row = jnp.where(part_left, part_row, part_row - edge)
-    is_own = jnp.where(part_left, edge - 1 - own_row, own_row) >= 0
-    is_own = is_own | (part_row >= 2 * edge)
-
-    def point_dot(left, right):
+    left_own = jnp.where(low_row | (row_of >= 2 * edge), 1.0, 0.0)
+    right_own = jnp.where(low_row, 0.0, 1.0)
+    owned = (jnp.where(even, left_own, right_own), jnp.where(even, right_own, left_own))
+
+    def point_part(left, right, side):
         running = left[0] * right[0]
         for index in range(1, 3):
             running = running + left[index] * right[index]
-        running = jnp.where(is_own, running, 0.0)
-        running = running[:, :LANES] + running[:, LANES:]
-        running = jnp.sum(running, axis=0, keepdims=True)
+        return running * owned[side]
+
+    def summed(tile):
+        running = jnp.sum(tile, axis=0, keepdims=True)
         return jnp.broadcast_to(jnp.sum(running, axis=1, keepdims=True), (1, LANES))
 
     def dots_copy(offset):
@@ -415,16 +418,16 @@
 
     chains = [None, None]
     for top in range(0, cams, GROUP):
-        near = slice(top, top + GROUP)
+        eight = slice(top, top + GROUP)
 
         def upper(ref, index):
-            return ref[index].astype(F32)[near]
+            return ref[index].astype(F32)[eight]
 
         errors = []
         for side in range(2):
-            running = upper(cam_jac, 9 * side) * start_col[0][near]
+            running = upper(cam_jac, 9 * side) * start_col[0][eight]
             for entry in range(1, 9):
-                running = running + upper(cam_jac, 9 * side + entry) * start_col[entry][near]
+                running = running + upper(cam_jac, 9 * side + entry) * start_col[entry][eight]
             errors.append(running)
         ours = [upper(point_jac, index) for index in range(6)]
         blocks = [ours[lead] * ours[tail] + ours[3 + lead] * ours[3 + tail] for lead, tail in ENTRY_PAIRS]
@@ -433,7 +436,7 @@
         ]
         for index, block in enumerate(blocks):
             for step, term in enumerate(splits_of(block)):
-                first_terms[SPLITS * index + step, near] = term
+                first_terms[SPLITS * index + step, eight] = term
         for cam in range(top, top + GROUP):
             side = 0 if cam % 2 == 0 or cam % 8 == 3 else 1
             if side == 0 and cam not in (0, 2):
@@ -443,9 +446,14 @@
             before = chains[side]
             chains[side] = part if before is None else before + part
     for index in range(9):
-        coupling[index] = joined(chains[0], index)
+        half_sum = joined(chains[0], index)
+        coupling[0, index], coupling[1, index] = half_sum[:, :LANES], half_sum[:, LANES:]
     whole = chains[1]
-    sums = [joined(whole, index) + coupling[index] for index in range(9)]
+    sums = [
+        joined(whole, index)
+        + jnp.concatenate([coupling[0, index], coupling[1, index]], axis=1)
+        for index in range(9)
+    ]
 
     moved = [point_damp[:, part * LANES : (part + 1) * LANES] for part in range(GROUP)]
     moved = jnp.concatenate(moved, axis=0)
@@ -459,7 +467,7 @@
             (own, jnp.where(low_row, chosen, side), jnp.where(low_row, side, chosen))
         )
         rows = slice(index * kept, (index + 1) * kept)
-        to_next[rows], to_prev[rows] = tiles[-1][1][:kept], tiles[-1][2][:kept]
+        leaving[0, rows], leaving[1, rows] = tiles[-1][1][:kept], tiles[-1][2][:kept]
 
     pl.semaphore_wait(barrier, len(reaches) + jnp.where(has_prev, 1, 0))
     tell(0)
@@ -522,7 +530,7 @@
         left = left + jnp.where(row_of == 2 * edge, rest, 0.0)
         moved = pltpu.roll(rest, GROUP - 1, 0)
         right_half = right_half + jnp.where(row_of == 2 * edge, moved, 0.0)
-        sums.append(jnp.concatenate([left, right_half], axis=1))
+        sums.append((jnp.where(even, left, right_half), jnp.where(even, right_half, left)))
 
     for top in range(0, cams, GROUP):
         for left in range(0, slots, LANES):
@@ -555,7 +563,9 @@
     for cam in range(cams):
         whole = scatter(terms, 27, cam)
         for index in range(27):
-            coupling[cam * 27 + index] = joined(whole, index)
+            both = joined(whole, index)
+            coupling[0, cam * 27 + index] = both[:, :LANES]
+            coupling[1, cam * 27 + index] = both[:, LANES:]
 
     precond = []
     for index, (lead, tail) in enumerate(SQUARES):
@@ -575,8 +585,13 @@
     start_image = square_product(start)
 
     hear(0)
-    sums = receive(sums, 0)
-    inverse = symmetric_inverse(sums[:6])
+    inverse = []
+    for side in range(2):
+        whole = arrived(sums, 0, side)
+        inverse.append(symmetric_inverse(whole[:6]))
+        values = apply_inverse(inverse[side], whole[6:])
+        if side == 0:
+            near_products(values)
     residual, direction = [], []
 
     def first_use(entry, back):
@@ -584,13 +599,16 @@
         direction.append(precond[entry] * residual[entry])
         return direction[entry]
 
-    sums = there_and_back(apply_inverse(inverse, sums[6:]), first_use)
+    sums = there_and_back(values, first_use)
     send(sums, 1)
     hear(1)
     square_direction = square_product(direction)
+    points_now = [arrived(sums, 1, 0)]
+    values = [apply_inverse(inverse[0], points_now[0])]
+    near_products(values[0])
     hear(2)
-    sums = receive(sums, 1)
-    values = apply_inverse(inverse, sums)
+    points_now.append(arrived(sums, 1, 1))
+    values.append(apply_inverse(inverse[1], points_now[1]))
     image, ahead = [], []
 
     def second_use(entry, back):
@@ -598,7 +616,7 @@
         ahead.append(precond[entry] * image[entry])
         return ahead[entry]
 
-    sums_ahead = there_and_back(values, second_use)
+    sums_ahead = there_and_back(values[1], second_use)
     send(sums_ahead, 2)
     hear(3)
     square_ahead = square_product(ahead)
@@ -628,18 +646,22 @@
     dots_out[1] = shift
     for turn in range(4, len(reaches)):
         hear(turn)
-    sums_ahead = receive(sums_ahead, 2)
-    values_ahead = apply_inverse(inverse, sums_ahead)
-    wide_shift = jnp.concatenate([shift] * halves, axis=1)
-    sums_rest = [sums[index] - wide_shift * sums_ahead[index] for index in range(3)]
-    values_rest = [values[index] - wide_shift * values_ahead[index] for index in range(3)]
-    packed = packed - jnp.where(dot_lane == 3, point_dot(sums_rest, values_rest), 0.0)
-    packed = packed - jnp.where(dot_lane == 6, 2.0 * point_dot(sums_rest, values_ahead), 0.0)
-    packed = packed - jnp.where(dot_lane == 9, point_dot(sums_ahead, values_ahead), 0.0)
+    values_ahead, tiles = [], [[], [], []]
+    for side in range(2):
+        points_ahead = arrived(sums_ahead, 2, side)
+        values_ahead.append(apply_inverse(inverse[side], points_ahead))
+        points_rest = [points_now[side][index] - shift * points_ahead[index] for index in range(3)]
+        values_rest = [values[side][index] - shift * values_ahead[side][index] for index in range(3)]
+        tiles[0].append(point_part(points_rest, values_rest, side))
+        tiles[1].append(point_part(points_rest, values_ahead[side], side))
+        tiles[2].append(point_part(points_ahead, values_ahead[side], side))
+    for lane, factor, pair in zip((3, 6, 9), (1.0, 2.0, 1.0), tiles):
+        packed = packed - jnp.where(dot_lane == lane, factor * summed(pair[0] + pair[1]), 0.0)
     dots_out[0] = packed
     lax.fori_loop(1, n, start_dots, 0)
 
-    further = [square_ahead[entry] - camera_entry(values_ahead, entry) for entry in range(9)]
+    near_products(values_ahead[0])
+    further = [square_ahead[entry] - camera_entry(values_ahead[1], entry) for entry in range(9)]
 
     def lines(vector):
         return jnp.concatenate([line(member) for member in vector], axis=0)
@@ -724,14 +746,12 @@
                 pltpu.VMEM((18, cams, slots), F32),
                 pltpu.VMEM((SPLITS * 9, cams, slots), F32),
                 pltpu.VMEM((SPLITS * 27, cams, slots), F32),
-                pltpu.VMEM((cams * 27, GROUP, WIDE), F32),
+                pltpu.VMEM((2, cams * 27, GROUP, LANES), F32),
                 pltpu.VMEM((9, cams * GROUP, LANES), F32),
                 pltpu.VMEM((9, cams, LANES), F32),
                 pltpu.VMEM((len(SQUARES), cams, LANES), F32),
-                pltpu.VMEM((link_rows, LANES), F32),
-                pltpu.VMEM((link_rows, LANES), F32),
-                pltpu.VMEM((link_rows, LANES), F32),
-                pltpu.VMEM((link_rows, LANES), F32),
+                pltpu.VMEM((2, link_rows, LANES), F32),
+                pltpu.VMEM((2, link_rows, LANES), F32),
                 pltpu.VMEM((2, 1, LANES), F32),
                 pltpu.VMEM((n - 1, 2, 1, LANES), F32),
                 pltpu.SemaphoreType.DMA((3,)),

time: 21.7 us -> 21.6 us (level)
  no operation moved by 1% of the time
where the time goes in v5:
time: 21.6 us; the launch traced here: 21.4 us
  Pallas kernels  20.2 us (94%)
  between operations  0.64 us (3%)
  local copies, waits for them, and re-layouts  0.61 us (3%)
    pallas_call x1, Pallas kernels, shards(): pl.pallas_call(functools.partial(kernel, n), out_shape=pltpu.VMEM((32, ri...  20.2 us
    slice x1, local copies, waits for them, and re-layouts, shards(): return (found[:9], found[16:25])  0.61 us

profile of v5, /device:TPU:0, one launch (start us, length us, event | category | flops | bytes accessed | tf_op | source)
XLA Modules:
  0.0 21.4 jit_solution(2158174253995140534)
XLA Ops:
  0.6 20.2 %schur_cg.1 = f32[32,16]{1,0:T(8,128)S(1)} custom-call(bf16[18,16,512]{2,1,0:T(8,128)(2,1)} %cam_jac_hbm.1, bf16[6,16,512]{2,1,0:T(8,128)(2,1)} %point_jac_hbm.1, s32[16,512]{1,0:T(8,128)} %obs_point_hbm.1, s32[1,16]{1,0:T(1,128)} %bitcast.4, s32[1,384]{1,0:T(1,128)} %back_list_hbm.1, s32[1,384]{1,0:T(1,128)} %front_list_hbm.1, f32[1,1024]{1,0:T(1,128)} %bitcast.3, ...), custom_call_target="tpu_custom_call" | custom-call | tf_op jit(solution)/shard_map/schur_cg/pallas_call | solution.py:738
  20.8 0.6 %fusion = (f32[9,16]{1,0:T(8,128)}, f32[9,16]{1,0:T(8,128)}) fusion(f32[32,16]{1,0:T(8,128)S(1)} %schur_cg.1), kind=kLoop, calls=%fused_computation | loop fusion | bytes 2304 | tf_op jit(solution)/shard_map/slice | solution.py:772

commit v6 on v5

--- a/solution.py
+++ b/solution.py
@@ -288,12 +288,30 @@
     far = 1 - near
     edge_row = row_of < 2 * edge
 
-    def send(sums, turn):
-        for index, member in enumerate(sums):
+    def start_next(turn, when):
+        @pl.when(jnp.logical_and(has_next, when))
+        def _():
+            neighbour("next", turn).start()
+
+    def start_prev(turn, when):
+        @pl.when(jnp.logical_and(has_prev, when))
+        def _():
+            neighbour("prev", turn).start()
+
+    def store_half(half, tiles, turn):
+        for index, tile in enumerate(tiles):
             rows = slice(spots[turn] + index * GROUP, spots[turn] + (index + 1) * GROUP)
-            leaving[near, rows] = member[0]
-            leaving[far, rows] = member[1]
-        start_pair(turn)
+            leaving[half, rows] = tile
+
+    def send_far(tiles, turn):
+        store_half(far, tiles, turn)
+        start_next(turn, jnp.logical_not(even))
+        start_prev(turn, even)
+
+    def send_near(tiles, turn):
+        store_half(near, tiles, turn)
+        start_next(turn, even)
+        start_prev(turn, jnp.logical_not(even))
 
     def wait_next(turn, when):
         @pl.when(jnp.logical_and(has_next, when))
@@ -324,15 +342,15 @@
     def spread_out(col):
         return jnp.broadcast_to(col, (cams, LANES))
 
-    def point_terms(running, entry, vector):
-        vector_rows[entry] = vector
-        for cam in range(cams):
-            scale = jnp.broadcast_to(vector_rows[entry, cam : cam + 1], (GROUP, LANES))
-            for index in range(3):
-                for side, half in enumerate((near, far)):
+    def point_half(half):
+        running = [None] * 3
+        for entry in range(9):
+            for cam in range(cams):
+                scale = jnp.broadcast_to(vector_rows[entry, cam : cam + 1], (GROUP, LANES))
+                for index in range(3):
                     term = coupling[half, cam * 27 + index * 9 + entry] * scale
-                    before = running[index][side]
-                    running[index][side] = term if before is None else before + term
+                    running[index] = term if running[index] is None else running[index] + term
+        return running
 
     def near_products(values):
         for entry in range(9):
@@ -354,11 +372,14 @@
             whole = whole + partial[entry, pl.ds(row, cams, stride=GROUP)]
         return spread_out(jnp.sum(whole, axis=1, keepdims=True))
 
-    def there_and_back(values, use):
-        running = [[None] * halves for index in range(3)]
+    def there_and_back(values, use, turn):
         for entry in range(9):
-            point_terms(running, entry, use(entry, camera_entry(values, entry)))
-        return running
+            vector_rows[entry] = use(entry, camera_entry(values, entry))
+        beyond = point_half(far)
+        send_far(beyond, turn)
+        inside = point_half(near)
+        send_near(inside, turn)
+        return list(zip(inside, beyond))
 
     def square_product(vector):
         result = [None] * 9
@@ -599,8 +620,7 @@
         direction.append(precond[entry] * residual[entry])
         return direction[entry]
 
-    sums = there_and_back(values, first_use)
-    send(sums, 1)
+    sums = there_and_back(values, first_use, 1)
     hear(1)
     square_direction = square_product(direction)
     points_now = [arrived(sums, 1, 0)]
@@ -616,8 +636,7 @@
         ahead.append(precond[entry] * image[entry])
         return ahead[entry]
 
-    sums_ahead = there_and_back(values[1], second_use)
-    send(sums_ahead, 2)
+    sums_ahead = there_and_back(values[1], second_use, 2)
     hear(3)
     square_ahead = square_product(ahead)
     inner = dot_of(residual, direction)

time: 21.6 us -> 21.4 us (level)
  no operation moved by 1% of the time
where the time goes in v6:
time: 21.4 us; the launch traced here: 21.2 us
  Pallas kernels  20 us (93%)
  between operations  0.64 us (3%)
  local copies, waits for them, and re-layouts  0.61 us (3%)
    pallas_call x1, Pallas kernels, shards(): pl.pallas_call(functools.partial(kernel, n), out_shape=pltpu.VMEM((32, ri...  20 us
    slice x1, local copies, waits for them, and re-layouts, shards(): return (found[:9], found[16:25])  0.61 us

profile of v6, /device:TPU:0, one launch (start us, length us, event | category | flops | bytes accessed | tf_op | source)
XLA Modules:
  0.0 21.2 jit_solution(7135762379223497455)
XLA Ops:
  0.6 20.0 %schur_cg.1 = f32[32,16]{1,0:T(8,128)S(1)} custom-call(bf16[18,16,512]{2,1,0:T(8,128)(2,1)} %cam_jac_hbm.1, bf16[6,16,512]{2,1,0:T(8,128)(2,1)} %point_jac_hbm.1, s32[16,512]{1,0:T(8,128)} %obs_point_hbm.1, s32[1,16]{1,0:T(1,128)} %bitcast.4, s32[1,384]{1,0:T(1,128)} %back_list_hbm.1, s32[1,384]{1,0:T(1,128)} %front_list_hbm.1, f32[1,1024]{1,0:T(1,128)} %bitcast.3, ...), custom_call_target="tpu_custom_call" | custom-call | tf_op jit(solution)/shard_map/schur_cg/pallas_call | solution.py:757
  20.6 0.6 %fusion = (f32[9,16]{1,0:T(8,128)}, f32[9,16]{1,0:T(8,128)}) fusion(f32[32,16]{1,0:T(8,128)S(1)} %schur_cg.1), kind=kLoop, calls=%fused_computation | loop fusion | bytes 2304 | tf_op jit(solution)/shard_map/slice | solution.py:791

commit v7 on v6

--- a/solution.py
+++ b/solution.py
@@ -95,11 +95,8 @@
     landing,
     dots_out,
     dots_in,
-    next_send,
     next_recv,
-    prev_send,
     prev_recv,
-    dots_send,
     dots_recv,
     told,
     cam_jac,
@@ -250,7 +247,7 @@
             return pltpu.make_async_remote_copy(
                 src_ref=leaving.at[0, pl.ds(spot, size)],
                 dst_ref=landing.at[1, pl.ds(spot, size)],
-                send_sem=next_send.at[turn],
+                send_sem=load_sem.at[turn],
                 recv_sem=next_recv.at[turn],
                 device_id=(lax.rem(me + 1, n),),
                 device_id_type=MESH,
@@ -258,7 +255,7 @@
         return pltpu.make_async_remote_copy(
             src_ref=leaving.at[1, pl.ds(spot, size)],
             dst_ref=landing.at[0, pl.ds(spot, size)],
-            send_sem=prev_send.at[turn],
+            send_sem=load_sem.at[3 + turn],
             recv_sem=prev_recv.at[turn],
             device_id=(lax.rem(me + n - 1, n),),
             device_id_type=MESH,
@@ -274,15 +271,6 @@
             start = jnp.where(tile_row == row, found, start)
         return start
 
-    def start_pair(turn):
-        @pl.when(has_next)
-        def _():
-            neighbour("next", turn).start()
-
-        @pl.when(has_prev)
-        def _():
-            neighbour("prev", turn).start()
-
     even = (me & 1) == 0
     near = me & 1
     far = 1 - near
@@ -298,6 +286,14 @@
         def _():
             neighbour("prev", turn).start()
 
+    def start_far(turn):
+        start_next(turn, jnp.logical_not(even))
+        start_prev(turn, even)
+
+    def start_near(turn):
+        start_next(turn, even)
+        start_prev(turn, jnp.logical_not(even))
+
     def store_half(half, tiles, turn):
         for index, tile in enumerate(tiles):
             rows = slice(spots[turn] + index * GROUP, spots[turn] + (index + 1) * GROUP)
@@ -305,13 +301,11 @@
 
     def send_far(tiles, turn):
         store_half(far, tiles, turn)
-        start_next(turn, jnp.logical_not(even))
-        start_prev(turn, even)
+        start_far(turn)
 
     def send_near(tiles, turn):
         store_half(near, tiles, turn)
-        start_next(turn, even)
-        start_prev(turn, jnp.logical_not(even))
+        start_near(turn)
 
     def wait_next(turn, when):
         @pl.when(jnp.logical_and(has_next, when))
@@ -415,7 +409,7 @@
         return pltpu.make_async_remote_copy(
             src_ref=dots_out,
             dst_ref=dots_in.at[offset - 1],
-            send_sem=dots_send,
+            send_sem=load_sem.at[6],
             recv_sem=dots_recv,
             device_id=(lax.rem(me + offset, n),),
             device_id_type=MESH,
@@ -487,12 +481,15 @@
         tiles.append(
             (own, jnp.where(low_row, chosen, side), jnp.where(low_row, side, chosen))
         )
-        rows = slice(index * kept, (index + 1) * kept)
-        leaving[0, rows], leaving[1, rows] = tiles[-1][1][:kept], tiles[-1][2][:kept]
 
     pl.semaphore_wait(barrier, len(reaches) + jnp.where(has_prev, 1, 0))
     tell(0)
-    start_pair(0)
+    for half, begin in ((far, start_far), (near, start_near)):
+        for index, (own, left, right_half) in enumerate(tiles):
+            first, other = (right_half, left) if half is far else (left, right_half)
+            tile = jnp.where(even, first, other)
+            leaving[half, index * kept : (index + 1) * kept] = tile[:kept]
+        begin(0)
 
     for index in range(18):
         wide_jac[index] = jnp.where(used, cam_jac[index].astype(F32), 0.0)
@@ -690,7 +687,7 @@
     )
 
     pltpu.make_async_copy(dots_in, dots_in, dots_recv).wait()
-    pltpu.make_async_copy(dots_in, dots_in, dots_send).wait()
+    pltpu.make_async_copy(dots_in, dots_in, load_sem.at[6]).wait()
 
     def picked(row, lane):
         wide = jnp.broadcast_to(row, (GROUP, LANES))
@@ -775,9 +772,6 @@
                 pltpu.VMEM((n - 1, 2, 1, LANES), F32),
                 pltpu.SemaphoreType.DMA((3,)),
                 pltpu.SemaphoreType.DMA((3,)),
-                pltpu.SemaphoreType.DMA((3,)),
-                pltpu.SemaphoreType.DMA((3,)),
-                pltpu.SemaphoreType.DMA,
                 pltpu.SemaphoreType.DMA,
                 pltpu.SemaphoreType.REGULAR((max(1, (n - 1).bit_length()),)),
                 *[pltpu.VMEM(member.shape, member.dtype) for member in operands],

time: 21.4 us -> 21.3 us (level)
  no operation moved by 1% of the time
where the time goes in v7:
time: 21.3 us; the launch traced here: 21.2 us
  Pallas kernels  19.9 us (93%)
  between operations  0.64 us (3%)
  local copies, waits for them, and re-layouts  0.61 us (3%)
    pallas_call x1, Pallas kernels, shards(): pl.pallas_call(functools.partial(kernel, n), out_shape=pltpu.VMEM((32, ri...  19.9 us
    slice x1, local copies, waits for them, and re-layouts, shards(): return (found[:9], found[16:25])  0.61 us

profile of v7, /device:TPU:0, one launch (start us, length us, event | category | flops | bytes accessed | tf_op | source)
XLA Modules:
  0.0 21.2 jit_solution(18365340701904452317)
XLA Ops:
  0.6 19.9 %schur_cg.1 = f32[32,16]{1,0:T(8,128)S(1)} custom-call(bf16[18,16,512]{2,1,0:T(8,128)(2,1)} %cam_jac_hbm.1, bf16[6,16,512]{2,1,0:T(8,128)(2,1)} %point_jac_hbm.1, s32[16,512]{1,0:T(8,128)} %obs_point_hbm.1, s32[1,16]{1,0:T(1,128)} %bitcast.4, s32[1,384]{1,0:T(1,128)} %back_list_hbm.1, s32[1,384]{1,0:T(1,128)} %front_list_hbm.1, f32[1,1024]{1,0:T(1,128)} %bitcast.3, ...), custom_call_target="tpu_custom_call" | custom-call | tf_op jit(solution)/shard_map/schur_cg/pallas_call | solution.py:754
  20.5 0.6 %fusion = (f32[9,16]{1,0:T(8,128)}, f32[9,16]{1,0:T(8,128)}) fusion(f32[32,16]{1,0:T(8,128)S(1)} %schur_cg.1), kind=kLoop, calls=%fused_computation | loop fusion | bytes 2304 | tf_op jit(solution)/shard_map/slice | solution.py:785
